TPU v7x, 32 devices: a whole 2x2x4 slice. The times are simulated.
32 devices in a mesh: row: 4 (over z), col: 8 (over y, x, core).
Axes of the slice: x: 2, y: 2, z: 4, core: 2. Of those that a mesh axis runs over, the one named last changes fastest.
Arguments:
- pressure: float32 [128, 256, 512], P('row', 'col'), may hold values from -6 to 6
- cut_exponent: int32 [4, 8, 2], P('row', 'col'), may hold values from 0 to 3
- group_map: int32 [4, 8, 2], P('row', 'col'), may hold values from 0 to 15
Outputs:
- coeffs: float32 [128, 256, 512], P('row', 'col')
- group_mass: float32 [16, 4], replicated
Inputs may be any that keep to these rules, and one draw needn't show every extreme that they name: `cut_exponent`: one exponent per block of 32 x 32 x 512 // 2 cells.
All inputs are finite; a program needn't handle non-finite values.
Results may differ from a plain program's by a relative error of at most 0.0001.
Values sent between devices are 32-bit elements; how exact they have to be, the bound alone decides.
A program may use at most 64 MiB of HBM per device.

v0:
```python
import functools

import jax
import jax.numpy as jnp
import numpy as np
from jax import lax
from jax.experimental import pallas as pl
from jax.experimental.pallas import tpu as pltpu
from jax.sharding import PartitionSpec as P

GROUPS = 16
LEVELS = (0.25, 0.5, 1.0, 2.0)
MESH = pl.DeviceIdType.MESH
F32, BF16 = jnp.float32, jnp.bfloat16


def cyclic_matrix(n):
    half = n // 2
    ev, od = np.eye(n)[0::2], np.eye(n)[1::2]
    r = lambda a, k: np.roll(a, k, 0)
    d = od - (0.5625 * (ev + r(ev, -1)) - 0.0625 * (r(ev, 1) + r(ev, -2)))
    s = ev + (0.28125 * (r(d, 1) + d) - 0.03125 * (r(d, 2) + r(d, -1)))
    return np.stack([s, d], 1).reshape(n, n) if half else None


def local_matrix(n):
    half = n // 2
    t = np.eye(n + 6)
    v, (a, b, c, f0, f1, g) = t[:n], t[n:]
    e = {j: v[2 * j] for j in range(half)}
    o = {j: v[2 * j + 1] for j in range(half)}
    e[-1], e[half], e[half + 1] = a, f0, f1
    d = {
        j: o[j] - 0.5625 * (e[j] + e[j + 1]) + 0.0625 * (e[j - 1] + e[j + 2])
        for j in range(half)
    }
    d[-1] = b - 0.5625 * e[0] + 0.0625 * e[1]
    d[-2] = c + 0.0625 * e[0]
    d[half] = g + 0.0625 * e[half - 1]
    out = np.zeros((n, n + 6))
    for j in range(half):
        out[2 * j] = e[j] + 0.28125 * (d[j - 1] + d[j]) - 0.03125 * (d[j - 2] + d[j + 1])
        out[2 * j + 1] = d[j]
    return out


def partials_low(row, n):
    a = row(n - 2)
    b = row(n - 1) - 0.5625 * a + 0.0625 * row(n - 4)
    c = row(n - 3) - 0.5625 * (row(n - 4) + a) + 0.0625 * row(n - 6)
    return a, b, c


def partials_high(row):
    f0, f1 = row(0), row(2)
    return f0, f1, row(1) - 0.5625 * (f0 + f1) + 0.0625 * row(4)


def split(value):
    hi = value.astype(BF16)
    return hi, (value - hi.astype(F32)).astype(BF16)


def dot2(left, right):
    dot = functools.partial(jnp.dot, preferred_element_type=F32)
    if left.dtype == BF16:
        hi, lo = split(right)
        return dot(left, hi) + dot(left, lo)
    hi, lo = split(left)
    return dot(hi, right) + dot(lo, right)


def kernel(
    n_row, n_col, grp, cut_hbm, map_hbm, p_ref, *refs
):
    weights, refs = refs[:6], refs[6:]
    out_hbm, mass_ref = refs[:2]
    ext, q, sx, su, u, sc, cb, part, slots, out_ref, cut_ref, map_ref = refs[2:14]
    held = refs[14:20]
    ws_ref, wy_ref, wu_ref, wx_ref, wc_ref, wz_ref = held
    in_sem, o_sem, w_sem, h_send, h_recv, g_send, g_recv, hop_sem = refs[20:]
    nx, ny, nz = p_ref.shape
    devices = n_row * n_col
    row, col = lax.axis_index("row"), lax.axis_index("col")
    me = row * n_col + col
    up_r, dn_r = lax.rem(row + 1, n_row), lax.rem(row + n_row - 1, n_row)
    up_c, dn_c = lax.rem(col + 1, n_col), lax.rem(col + n_col - 1, n_col)

    def wrap(value, size):
        return lax.select(value >= size, value - size, value)

    def peers(visit):
        @pl.loop(1, n_row)
        def _(j):
            other = wrap(row + j, n_row)

            @pl.loop(0, n_col)
            def _(k):
                visit(other, wrap(col + k, n_col))

        @pl.loop(1, n_col)
        def _(k):
            visit(row, wrap(col + k, n_col))

    barrier = pltpu.get_barrier_semaphore()

    def greet(r, c):
        pl.semaphore_signal(barrier, inc=1, device_id=(r, c), device_id_type=MESH)

    for r, c in ((up_r, col), (dn_r, col), (row, up_c), (row, dn_c)):
        greet(r, c)
    pieces = ((0, 8), (nx - 8, 8), (8, nx - 16))
    loads = []
    for i, (at, size) in enumerate(pieces):
        load = pltpu.make_async_copy(
            p_ref.at[pl.ds(at, size)], ext.at[pl.ds(at, size)], in_sem.at[i]
        )
        load.start()
        loads.append(load)

    fetched = []
    for i, (src, dst) in enumerate(
        zip((*weights, cut_hbm, map_hbm), (*held, cut_ref, map_ref), strict=True)
    ):
        fetch = pltpu.make_async_copy(src, dst, w_sem.at[i])
        fetch.start()
        fetched.append(fetch)

    along_col = max(n_col // 2 - 1, 1)
    hops = along_col + n_row // 2

    def call(k):
        aim = ((row, up_c), (row, dn_c)) if k < along_col else ((up_r, col), (dn_r, col))
        for to in aim:
            pl.semaphore_signal(hop_sem.at[k], inc=1, device_id=to, device_id_type=MESH)

    def relay(k):
        pl.semaphore_wait(hop_sem.at[k], 2)
        if k + 1 < hops:
            call(k + 1)


    sends = []

    def send(src, dst, to):
        i = len(sends)
        copy = pltpu.make_async_remote_copy(
            src_ref=src, dst_ref=dst, send_sem=h_send.at[i], recv_sem=h_recv.at[i],
            device_id=to, device_id_type=MESH,
        )
        copy.start()
        sends.append(copy)

    loads[0].wait()
    loads[1].wait()
    _, b, c = partials_low(lambda i: ext[i], nx)
    sx[0], sx[1] = b, c
    sx[2] = partials_high(lambda i: ext[i])[2]
    loads[2].wait()
    for fetch in fetched:
        fetch.wait()
    for g in range(nx // grp):
        at = pl.ds(g * grp, grp)
        got = dot2(ws_ref[...], ext[at].reshape(grp * ny, nz))
        su[:, at, :] = got.reshape(6, grp, nz)
    for d in range(4):
        for k in range(3):
            plane = (d % 2) * 3 + k
            x_row = lambda i: su[plane, pl.ds(i, 1), :]
            got = partials_low(x_row, nx) if d < 2 else partials_high(x_row)
            for i in range(3):
                sc[9 * d + 3 * i + k] = got[i]

    pl.semaphore_wait(barrier, 4)
    call(0)
    send(sx.at[pl.ds(0, 2)], ext.at[pl.ds(nx + 1, 2)], (up_r, col))
    send(sx.at[2], ext.at[nx + 5], (dn_r, col))
    send(ext.at[nx - 2], ext.at[nx], (up_r, col))
    send(ext.at[0], ext.at[nx + 3], (dn_r, col))
    send(ext.at[2], ext.at[nx + 4], (dn_r, col))
    send(su.at[pl.ds(0, 3)], u.at[pl.ds(0, 3)], (row, up_c))
    send(su.at[pl.ds(3, 3)], u.at[pl.ds(3, 3)], (row, dn_c))
    relay(0)
    for d in range(4):
        to = (up_r if d < 2 else dn_r, up_c if d % 2 == 0 else dn_c)
        send(sc.at[pl.ds(9 * d, 9)], cb.at[pl.ds(9 * d, 9)], to)

    for g in range(nx // grp):
        at = pl.ds(g * grp, grp)
        q[at] = dot2(wy_ref[...], ext[at].reshape(grp * ny, nz)).reshape(grp, ny, nz)
    relay(1)
    for copy in sends[5:7]:
        copy.wait_recv()
    relay(2)
    for g in range(nx // grp):
        at = pl.ds(g * grp, grp)
        more = dot2(wu_ref[...], u[:, at, :].reshape(6 * grp, nz))
        q[at] += more.reshape(grp, ny, nz)
    half = nx // 2
    relay(3)

    def x_lift(low, high):
        @pl.loop(0, ny // 8)
        def _(t):
            rows = pl.ds(pl.multiple_of(t * 8, 8), 8)
            far = {-1: nx, half: nx + 3, half + 1: nx + 4}
            first, last = max(low - 3, -1), min(high + 2, half + 1)
            e = {j: q[far.get(j, 2 * j), rows, :] for j in range(first, last + 1)}

            def detail(j):
                if j == -1:
                    return q[nx + 1, rows, :] - 0.5625 * e[0] + 0.0625 * e[1]
                if j == -2:
                    return q[nx + 2, rows, :] + 0.0625 * e[0]
                if j == half:
                    return q[nx + 5, rows, :] + 0.0625 * e[half - 1]
                odd = q[2 * j + 1, rows, :]
                return odd - 0.5625 * (e[j] + e[j + 1]) + 0.0625 * (e[j - 1] + e[j + 2])

            d = {j: detail(j) for j in range(low - 2, low + 1)}
            for j in range(low, high):
                d[j + 1] = detail(j + 1)
                near, wide = d[j - 1] + d[j], d[j - 2] + d[j + 1]
                ext[2 * j, rows, :] = e[j] + 0.28125 * near - 0.03125 * wide
                ext[2 * j + 1, rows, :] = d[j]

    zb = cut_ref.shape[2]
    width = nz // zb
    cuts = jnp.concatenate(
        [jnp.full((1, width), -cut_ref[0, 0, z], jnp.int32) for z in range(zb)], 1
    )
    scale = jnp.exp2(cuts.astype(F32))
    limits = [level * scale for level in LEVELS]
    odd = lambda axis: lax.broadcasted_iota(jnp.int32, (8, nz), axis) % 2
    mixed = (odd(0) + odd(1)) > 0

    def z_group(g, totals):
        at = pl.ds(g * grp, grp)
        made = dot2(ext[at].reshape(grp * ny, nz), wz_ref[...])
        out_ref[at] = made.reshape(grp, ny, nz)
        pltpu.make_async_copy(out_ref.at[at], out_hbm.at[at], o_sem.at[g]).start()
        totals = list(totals)
        for i in range(grp * ny // 8):
            size = jnp.abs(made[8 * i : 8 * i + 8])
            if (8 * i // ny) % 2 == 0:
                size = jnp.where(mixed, size, 0.0)
            for n, limit in enumerate(limits):
                totals[n] += jnp.maximum(size - limit, 0.0)
        return tuple(totals)

    groups = nx // grp
    totals = tuple(jnp.zeros((8, nz), F32) for _ in LEVELS)
    x_lift(grp // 2, half - grp // 2)
    totals = lax.fori_loop(1, groups - 1, z_group, totals)
    for k in range(4, hops):
        relay(k)
    for copy in sends[:5] + sends[7:]:
        copy.wait_recv()
    for copy in sends:
        copy.wait_send()
    edge = dot2(wx_ref[...], ext[pl.ds(nx, 6)].reshape(6 * ny, nz))
    edge += dot2(wc_ref[...], cb[...].reshape(-1, nz))
    q[pl.ds(nx, 6)] = edge.reshape(6, ny, nz)
    x_lift(0, grp // 2)
    x_lift(half - grp // 2, half)
    for g in (0, groups - 1):
        totals = z_group(g, totals)
    lane = lax.broadcasted_iota(jnp.int32, (1, 128), 1)
    line = jnp.zeros((1, 128), F32)
    cells = nx * ny * width
    n_lev = len(LEVELS)
    for z in range(zb):
        for n in range(n_lev):
            mass = jnp.sum(totals[n][:, z * width : (z + 1) * width], keepdims=True) / cells
            line += jnp.where(lane == n * GROUPS + map_ref[0, 0, z], mass, 0.0)
    part[...] = line
    slots[me] = line

    def spread(r, c):
        pltpu.make_async_remote_copy(
            src_ref=part, dst_ref=slots.at[me], send_sem=g_send.at[r * n_col + c],
            recv_sem=g_recv.at[me], device_id=(r, c), device_id_type=MESH,
        ).start()

    def gather(r, c):
        t = r * n_col + c
        pltpu.make_async_remote_copy(
            src_ref=part, dst_ref=slots.at[t], send_sem=g_send.at[t],
            recv_sem=g_recv.at[t], device_id=(r, c), device_id_type=MESH,
        ).wait()

    peers(spread)
    peers(gather)
    for g in range(groups):
        at = pl.ds(g * grp, grp)
        pltpu.make_async_copy(out_ref.at[at], out_hbm.at[at], o_sem.at[g]).wait()

    total = jnp.sum(slots[...], axis=0)
    mass_ref[...] = jnp.concatenate(
        [total[:, n * GROUPS : (n + 1) * GROUPS] for n in range(n_lev)], 0
    )


def deliver(c_hbm, m_hbm, out_hbm, mass_hbm, held, line, sems, m_sems):
    count = sems.shape[1]
    size = held.shape[0] // count
    piece = [pl.ds(i * size, size) for i in range(count)]
    copy = pltpu.make_async_copy
    ins = [copy(c_hbm.at[p], held.at[p], sems.at[0, i]) for i, p in enumerate(piece)]
    outs = [copy(held.at[p], out_hbm.at[p], sems.at[1, i]) for i, p in enumerate(piece)]
    ins.insert(1, copy(m_hbm, line, m_sems.at[0]))
    outs.insert(1, copy(line, mass_hbm, m_sems.at[1]))
    for c in ins:
        c.start()
    for c, o in zip(ins, outs, strict=True):
        c.wait()
        o.start()
    for o in outs:
        o.wait()


def solution(mesh):
    n_row, n_col = mesh.shape["row"], mesh.shape["col"]

    def shards(pressure, cut_exponent, group_map):
        nx, ny, nz = pressure.shape
        grp = 8
        devices = n_row * n_col
        local = local_matrix(ny)
        wy = np.kron(np.eye(grp), local[:, :ny])
        wu = np.einsum("xw,yk->xykw", np.eye(grp), local[:, ny:]).reshape(grp * ny, 6 * grp)
        eye = np.eye(ny)
        row = lambda i: eye[i]
        near = np.stack(partials_low(row, ny) + partials_high(row))
        ws = np.einsum("ky,xw->kxwy", near, np.eye(grp)).reshape(6 * grp, grp * ny)
        wx = np.kron(np.eye(6), local[:, :ny])
        wc = np.zeros((6, ny, 4, 9))
        for d in range(4):
            for i in range(3):
                for k in range(3):
                    wc[(d // 2) * 3 + i, :, d, 3 * i + k] = local[:, ny + (d % 2) * 3 + k]
        wc = wc.reshape(6 * ny, 36)
        weights = [jnp.asarray(w, BF16) for w in (ws, wy, wu, wx, wc, cyclic_matrix(nz).T)]
        vmem = pl.BlockSpec(memory_space=pltpu.VMEM)
        hbm = pl.BlockSpec(memory_space=pl.ANY)
        found = pl.pallas_call(
            functools.partial(kernel, n_row, n_col, grp),
            out_shape=(
                jax.ShapeDtypeStruct((nx, ny, nz), F32),
                jax.ShapeDtypeStruct((len(LEVELS), GROUPS), F32),
            ),
            in_specs=[hbm] * 9,
            out_specs=(hbm, vmem),
            scratch_shapes=[
                pltpu.VMEM((nx + 8, ny, nz), F32),
                pltpu.VMEM((nx + 6, ny, nz), F32),
                pltpu.VMEM((3, ny, nz), F32),
                pltpu.VMEM((6, nx, nz), F32),
                pltpu.VMEM((6, nx, nz), F32),
                pltpu.VMEM((36, 1, nz), F32),
                pltpu.VMEM((36, 1, nz), F32),
                pltpu.VMEM((1, 128), F32),
                pltpu.VMEM((devices, 1, 128), F32),
                pltpu.VMEM((nx, ny, nz), F32),
                pltpu.SMEM(cut_exponent.shape, jnp.int32),
                pltpu.SMEM(group_map.shape, jnp.int32),
                *(pltpu.VMEM(w.shape, BF16) for w in weights),
                pltpu.SemaphoreType.DMA((3,)),
                pltpu.SemaphoreType.DMA((nx // grp,)),
                pltpu.SemaphoreType.DMA((8,)),
                pltpu.SemaphoreType.DMA((11,)),
                pltpu.SemaphoreType.DMA((11,)),
                pltpu.SemaphoreType.DMA((devices,)),
                pltpu.SemaphoreType.DMA((devices,)),
                pltpu.SemaphoreType.REGULAR((n_col // 2 + n_row // 2,)),
            ],
            compiler_params=pltpu.CompilerParams(
                collective_id=0, has_side_effects=True, vmem_limit_bytes=62 * 2**20
            ),
        )(cut_exponent, group_map, pressure, *weights)
        coeffs, mass = pl.pallas_call(
            deliver,
            out_shape=tuple(jax.ShapeDtypeStruct(f.shape, F32) for f in found),
            in_specs=[hbm] * 2,
            out_specs=(hbm, hbm),
            scratch_shapes=[
                pltpu.VMEM((nx, ny, nz), F32),
                pltpu.VMEM(found[1].shape, F32),
                pltpu.SemaphoreType.DMA((2, 8)),
                pltpu.SemaphoreType.DMA((2,)),
            ],
            compiler_params=pltpu.CompilerParams(vmem_limit_bytes=62 * 2**20),
        )(*found)
        return coeffs, mass.T

    specs = P("row", "col", None)
    return jax.shard_map(
        shards, mesh=mesh, in_specs=(specs,) * 3, out_specs=(specs, P()), check_vma=False
    )
```

profile of v0, /device:TPU:0, one launch (start us, length us, event | category | flops | bytes accessed | tf_op | source)
XLA Modules:
  0.0 29.0 jit_solution(10507710857274675626)
XLA Ops:
  0.6 25.7 %shard_map.104 = (f32[32,32,512]{2,1,0:T(8,128)}, f32[4,16]{1,0:T(4,128)}) custom-call(s32[1,1,2]{2,1,0:T(1,128)} %cut_hbm.1, s32[1,1,2]{2,1,0:T(1,128)} %map_hbm.1, f32[32,32,512]{2,1,0:T(8,128)} %p_ref.1, bf16[48,256]{1,0:T(8,128)(2,1)} %constant.12.clone.refs_0_, bf16[256,256]{1,0:T(8,128)(2,1)} %constant.13.clone.refs_1_, ...), custom_call_target="tpu_custom_call" | custom-call | tf_op jit(solution)/shard_map/pallas_call | solution.py:346
  26.4 2.6 %shard_map.105 = (f32[32,32,512]{2,1,0:T(8,128)}, f32[4,16]{1,0:T(4,128)}) custom-call(f32[32,32,512]{2,1,0:T(8,128)} %get-tuple-element.6.c_hbm, f32[4,16]{1,0:T(4,128)} %get-tuple-element.7.m_hbm), custom_call_target="tpu_custom_call" | custom-call | tf_op jit(solution)/shard_map/pallas_call | solution.py:381
where the time goes:
time: 29.2 us; the launch traced here: 29 us
  Pallas kernels  28.4 us (97%)
  between operations  0.64 us (2%)
    pallas_call x1, Pallas kernels, shards(): pl.pallas_call(functools.partial(kernel, n_row, n_col, grp), out_shape=(j...  25.7 us
    pallas_call x1, Pallas kernels, shards(): pl.pallas_call(deliver, out_shape=tuple((jax.ShapeDtypeStruct(f.shape, F3...  2.63 us

commit v1 on v0

v1 whole, which is shorter than its diff:
```python
import functools

import jax
import jax.numpy as jnp
import numpy as np
from jax import lax
from jax.experimental import pallas as pl
from jax.experimental.pallas import tpu as pltpu
from jax.sharding import PartitionSpec as P

GROUPS = 16
LEVELS = (0.25, 0.5, 1.0, 2.0)
MESH = pl.DeviceIdType.MESH
F32, BF16 = jnp.float32, jnp.bfloat16
TILE, LANES = 8, 128
UNROLL = 64


def cyclic_matrix(n):
    ev, od = np.eye(n)[0::2], np.eye(n)[1::2]
    r = lambda a, k: np.roll(a, k, 0)
    d = od - (0.5625 * (ev + r(ev, -1)) - 0.0625 * (r(ev, 1) + r(ev, -2)))
    s = ev + (0.28125 * (r(d, 1) + d) - 0.03125 * (r(d, 2) + r(d, -1)))
    return np.stack([s, d], 1).reshape(n, n)


def local_matrix(n):
    half = n // 2
    t = np.eye(n + 6)
    v, (a, b, c, f0, f1, g) = t[:n], t[n:]
    e = {j: v[2 * j] for j in range(half)}
    o = {j: v[2 * j + 1] for j in range(half)}
    e[-1], e[half], e[half + 1] = a, f0, f1
    d = {
        j: o[j] - 0.5625 * (e[j] + e[j + 1]) + 0.0625 * (e[j - 1] + e[j + 2])
        for j in range(half)
    }
    d[-1] = b - 0.5625 * e[0] + 0.0625 * e[1]
    d[-2] = c + 0.0625 * e[0]
    d[half] = g + 0.0625 * e[half - 1]
    out = np.zeros((n, n + 6))
    for j in range(half):
        out[2 * j] = e[j] + 0.28125 * (d[j - 1] + d[j]) - 0.03125 * (d[j - 2] + d[j + 1])
        out[2 * j + 1] = d[j]
    return out


def partials_low(row, n):
    a = row(n - 2)
    b = row(n - 1) - 0.5625 * a + 0.0625 * row(n - 4)
    c = row(n - 3) - 0.5625 * (row(n - 4) + a) + 0.0625 * row(n - 6)
    return a, b, c


def partials_high(row):
    f0, f1 = row(0), row(2)
    return f0, f1, row(1) - 0.5625 * (f0 + f1) + 0.0625 * row(4)


def split(value):
    hi = value.astype(BF16)
    return hi, (value - hi.astype(F32)).astype(BF16)


def dot2(left, right):
    dot = functools.partial(jnp.dot, preferred_element_type=F32)
    if left.dtype == BF16:
        hi, lo = split(right)
        return dot(left, hi) + dot(left, lo)
    hi, lo = split(left)
    return dot(hi, right) + dot(lo, right)


def doublings(n_row, n_col):
    hops, known = [], 1
    while known < n_col // 2:
        hops.append((1, known))
        known *= 2
    known = 0
    while known < n_row // 2:
        hops.append((0, max(known, 1)))
        known += max(known, 1)
    return hops


def kernel(n_row, n_col, grp, cut_hbm, map_hbm, p_ref, *refs):
    weights, refs = refs[:8], refs[8:]
    out_ref, mass_ref = refs[:2]
    ext, v, q, hs, h, su, u, sc, cb, part, slots, cut_ref, map_ref = refs[2:15]
    held = refs[15:23]
    ws_ref, wz_ref, wy_ref, wu_ref, wsa_ref, wxa_ref, wxb_ref, wc_ref = held
    in_sem, w_sem, h_send, h_recv, g_send, g_recv, hop_sem = refs[23:]
    nx, ny, nz = p_ref.shape
    half = nx // 2
    devices = n_row * n_col
    row, col = lax.axis_index("row"), lax.axis_index("col")
    me = row * n_col + col
    away_r = lambda k: lax.rem(row + (k + n_row), n_row)
    away_c = lambda k: lax.rem(col + (k + n_col), n_col)
    up_r, dn_r, up_c, dn_c = away_r(1), away_r(-1), away_c(1), away_c(-1)

    barrier = pltpu.get_barrier_semaphore()
    for r, c in ((up_r, col), (dn_r, col), (row, up_c), (row, dn_c)):
        pl.semaphore_signal(barrier, inc=1, device_id=(r, c), device_id_type=MESH)

    loads = []
    starts = [0, nx - grp, *range(grp, nx - grp, grp)]
    for i, at in enumerate(starts):
        load = pltpu.make_async_copy(
            p_ref.at[pl.ds(at, grp)], ext.at[pl.ds(at, grp)], in_sem.at[i]
        )
        load.start()
        loads.append(load)
    fetched = []
    for i, (src, dst) in enumerate(
        zip((*weights, cut_hbm, map_hbm), (*held, cut_ref, map_ref), strict=True)
    ):
        fetch = pltpu.make_async_copy(src, dst, w_sem.at[i])
        fetch.start()
        fetched.append(fetch)

    hops = doublings(n_row, n_col)

    def call(k):
        axis, far = hops[k]
        if axis:
            aim = ((row, away_c(far)), (row, away_c(-far)))
        else:
            aim = ((away_r(far), col), (away_r(-far), col))
        for to in aim:
            pl.semaphore_signal(hop_sem.at[k], inc=1, device_id=to, device_id_type=MESH)

    def relay(k):
        if k < len(hops):
            pl.semaphore_wait(hop_sem.at[k], 2)
            if k + 1 < len(hops):
                call(k + 1)

    sends = []

    def send(src, dst, to):
        i = len(sends)
        copy = pltpu.make_async_remote_copy(
            src_ref=src, dst_ref=dst, send_sem=h_send.at[i], recv_sem=h_recv.at[i],
            device_id=to, device_id_type=MESH,
        )
        copy.start()
        sends.append(copy)
        return copy

    with jax.named_scope("ld01"):
        loads[0].wait()
        loads[1].wait()
    with jax.named_scope("hs"):
        for i, plane in enumerate(partials_low(lambda i: ext[i], nx) + partials_high(lambda i: ext[i])):
            hs[i] = plane
    with jax.named_scope("bar"):
        pl.semaphore_wait(barrier, 4)
    lo, hi = pl.ds(0, 3), pl.ds(3, 3)
    outer, inner = [], []
    for rows, kept in (
        (pl.ds(0, TILE), outer), (pl.ds(ny - TILE, TILE), outer),
        (pl.ds(TILE, ny - 2 * TILE), inner),
    ):
        kept.append(send(hs.at[lo, rows], h.at[lo, rows], (up_r, col)))
        kept.append(send(hs.at[hi, rows], h.at[hi, rows], (dn_r, col)))
    if hops:
        call(0)

    with jax.named_scope("su"):
        fetched[0].wait()
        near = []
        for i, at in enumerate(starts):
            if i > 1:
                loads[i].wait()
            at = pl.ds(at, grp)
            got = dot2(ws_ref[...], ext[at].reshape(grp * ny, nz))
            su[:, at, :] = got.reshape(6, grp, nz)
            near.append(send(su.at[lo, at], u.at[lo, at], (row, up_c)))
            near.append(send(su.at[hi, at], u.at[hi, at], (row, dn_c)))
    relay(0)
    groups = nx // grp
    with jax.named_scope("z"):
        fetched[1].wait()
        for g in range(groups):
            at = pl.ds(g * grp, grp)
            v[at] = dot2(ext[at].reshape(grp * ny, nz), wz_ref[...]).reshape(grp, ny, nz)
            if g == groups // 2 - 1:
                relay(1)
    relay(2)
    with jax.named_scope("y"):
        for fetch in fetched[2:]:
            fetch.wait()
        for g in range(groups):
            at = pl.ds(g * grp, grp)
            q[at] = dot2(wy_ref[...], v[at].reshape(grp * ny, nz)).reshape(grp, ny, nz)
    relay(3)
    with jax.named_scope("wait_u"):
        for copy in near:
            copy.wait_recv()
    with jax.named_scope("u"):
        zu = dot2(u[...].reshape(6 * nx, nz), wz_ref[...]).reshape(6, nx, nz)
        for g in range(groups):
            at = slice(g * grp, (g + 1) * grp)
            more = dot2(wu_ref[...], zu[:, at, :].reshape(6 * grp, nz))
            q[at] += more.reshape(grp, ny, nz)
    for k in range(4, len(hops)):
        relay(k)

    zb = cut_ref.shape[2]
    width = nz // zb
    n_lev = len(LEVELS)
    odd = lambda axis: lax.broadcasted_iota(jnp.int32, (TILE, LANES), axis) % 2
    mixed = (odd(0) + odd(1)) > 0

    def x_stage(totals, edges):
        totals = list(totals)
        for z in range(zb):
            cuts = jnp.full((TILE, LANES), -cut_ref[0, 0, z], jnp.int32)
            scale = jnp.exp2(cuts.astype(F32))
            limits = [level * scale for level in LEVELS]

            def tile(t, sums, z=z, limits=limits):
                rows = pl.ds(pl.multiple_of(t * TILE, TILE), TILE)
                sums = list(sums)
                for at in range(z * width, (z + 1) * width, LANES):
                    lanes = pl.ds(at, LANES)

                    def put(plane, value):
                        out_ref[plane, rows, lanes] = value
                        size = jnp.abs(value)
                        if plane % 2 == 0:
                            size = jnp.where(mixed, size, 0.0)
                        for n, limit in enumerate(limits):
                            sums[n] += jnp.maximum(size - limit, 0.0)

                    far = {-1: nx, half: nx + 3, half + 1: nx + 4}
                    e = lambda j: q[far.get(j, 2 * j), rows, lanes]

                    def detail(j):
                        if j == -1:
                            return q[nx + 1, rows, lanes] - 0.5625 * e(0) + 0.0625 * e(1)
                        if j == -2:
                            return q[nx + 2, rows, lanes] + 0.0625 * e(0)
                        if j == half:
                            return q[nx + 5, rows, lanes] + 0.0625 * e(half - 1)
                        return q[2 * j + 1, rows, lanes] - 0.5625 * (e(j) + e(j + 1)) + 0.0625 * (e(j - 1) + e(j + 2))

                    def smooth(d, j):
                        put(2 * j, e(j) + 0.28125 * (d[j - 1] + d[j]) - 0.03125 * (d[j - 2] + d[j + 1]))

                    if not edges:
                        d = {}
                        for j in range(1, half - 2):
                            d[j] = detail(j)
                            put(2 * j + 1, d[j])
                            if j >= 4:
                                smooth(d, j - 1)
                    else:
                        d = {j: out_ref[2 * j + 1, rows, lanes] for j in (1, 2, 3)}
                        d |= {j: detail(j) for j in (-2, -1, 0)}
                        put(1, d[0])
                        for j in (0, 1, 2):
                            smooth(d, j)
                        d = {j: out_ref[2 * j + 1, rows, lanes] for j in range(half - 5, half - 2)}
                        d |= {j: detail(j) for j in range(half - 2, half + 1)}
                        for j in (half - 2, half - 1):
                            put(2 * j + 1, d[j])
                        for j in range(half - 3, half):
                            smooth(d, j)
                return tuple(sums)

            mine = slice(z * n_lev, (z + 1) * n_lev)
            totals[mine] = lax.fori_loop(0, ny // TILE, tile, tuple(totals[mine]))
        return totals

    with jax.named_scope("wait_outer"):
        for copy in outer:
            copy.wait_recv()
    with jax.named_scope("corner"):
        rim = jnp.concatenate([h[:, :TILE, :], h[:, ny - TILE :, :]], 1).reshape(12 * TILE, nz)
        zrim = dot2(rim, wz_ref[...])
        sc[...] = dot2(wsa_ref[...], zrim).reshape(6, TILE, nz)
        corner = [
            send(sc.at[lo], cb.at[lo], (row, up_c)),
            send(sc.at[hi], cb.at[hi], (row, dn_c)),
        ]
        q[pl.ds(nx, 6)] = dot2(wxa_ref[...], zrim).reshape(6, ny, nz)
    with jax.named_scope("xin"):
        totals = [jnp.zeros((TILE, LANES), F32) for _ in range(zb * n_lev)]
        totals = x_stage(totals, False)
    with jax.named_scope("wait_inner"):
        for copy in inner:
            copy.wait_recv()
    with jax.named_scope("wait_corner"):
        for copy in corner:
            copy.wait_recv()
    with jax.named_scope("edge"):
        core = h[:, TILE : ny - TILE, :].reshape(6 * (ny - 2 * TILE), nz)
        edge = dot2(wxb_ref[...], dot2(core, wz_ref[...]))
        edge += dot2(wc_ref[...], cb[...].reshape(6 * TILE, nz))
        q[pl.ds(nx, 6)] += edge.reshape(6, ny, nz)
    with jax.named_scope("xedge"):
        totals = x_stage(totals, True)
    with jax.named_scope("line"):
        lane = lax.broadcasted_iota(jnp.int32, (1, LANES), 1)
        line = jnp.zeros((1, LANES), F32)
        cells = nx * ny * width
        for z in range(zb):
            for n in range(n_lev):
                mass = jnp.sum(totals[z * n_lev + n], keepdims=True) / cells
                line += jnp.where(lane == n * GROUPS + map_ref[0, 0, z], mass, 0.0)
        part[...] = line
        slots[me] = line

    def spread(r, c, t):
        return pltpu.make_async_remote_copy(
            src_ref=part, dst_ref=slots.at[me], send_sem=g_send.at[t],
            recv_sem=g_recv.at[me], device_id=(r, c), device_id_type=MESH,
        )

    def gather(r, c, t):
        return pltpu.make_async_remote_copy(
            src_ref=part, dst_ref=slots.at[t], send_sem=g_send.at[t],
            recv_sem=g_recv.at[t], device_id=(r, c), device_id_type=MESH,
        )

    def peers(visit):
        if devices <= UNROLL:
            for j in reversed(range(n_row)):
                for k in range(n_col):
                    if j or k:
                        r, c = away_r(j), away_c(k)
                        visit(r, c, r * n_col + c)
            return

        @pl.loop(1, n_row)
        def _(j):
            @pl.loop(0, n_col)
            def _(k):
                r, c = lax.rem(row + j, n_row), lax.rem(col + k, n_col)
                visit(r, c, r * n_col + c)

        @pl.loop(1, n_col)
        def _(k):
            c = lax.rem(col + k, n_col)
            visit(row, c, row * n_col + c)

    with jax.named_scope("spread"):
        peers(lambda r, c, t: spread(r, c, t).start())
    with jax.named_scope("wsend"):
        for copy in sends:
            copy.wait_send()
    with jax.named_scope("gather"):
        peers(lambda r, c, t: gather(r, c, t).wait())
    with jax.named_scope("sum"):
        total = jnp.sum(slots[...], axis=0)
        mass_ref[...] = jnp.concatenate(
            [total[:, n * GROUPS : (n + 1) * GROUPS] for n in range(n_lev)], 0
        )


def deliver(c_ref, m_ref, out_hbm, mass_hbm, sems, m_sem):
    count = sems.shape[0]
    size = c_ref.shape[0] // count
    copies = [pltpu.make_async_copy(m_ref, mass_hbm, m_sem)]
    for i in range(count):
        at = pl.ds(i * size, size)
        copies.append(pltpu.make_async_copy(c_ref.at[at], out_hbm.at[at], sems.at[i]))
    for copy in copies:
        copy.start()
    for copy in copies:
        copy.wait()


def solution(mesh):
    n_row, n_col = mesh.shape["row"], mesh.shape["col"]

    def shards(pressure, cut_exponent, group_map):
        nx, ny, nz = pressure.shape
        grp = 8
        devices = n_row * n_col
        local = local_matrix(ny)
        own, beyond = local[:, :ny], local[:, ny:]
        wy = np.kron(np.eye(grp), own)
        wu = np.einsum("xw,yk->xykw", np.eye(grp), beyond).reshape(grp * ny, 6 * grp)
        eye = np.eye(ny)
        take = lambda i: eye[i]
        near = np.stack(partials_low(take, ny) + partials_high(take))
        ws = np.einsum("ky,xw->kxwy", near, np.eye(grp)).reshape(6 * grp, grp * ny)
        rim = np.r_[0:TILE, ny - TILE : ny]
        six = np.eye(6, TILE).T
        wsa = np.einsum("ky,wp->kwpy", near[:, rim], six).reshape(6 * TILE, 6 * 2 * TILE)
        wxa = np.kron(np.eye(6), own[:, rim])
        wxb = np.kron(np.eye(6), own[:, TILE : ny - TILE])
        wc = np.einsum("wp,yk->pykw", six, beyond).reshape(6 * ny, 6 * TILE)
        weights = [
            jnp.asarray(w, BF16)
            for w in (ws, cyclic_matrix(nz).T, wy, wu, wsa, wxa, wxb, wc)
        ]
        vmem = pl.BlockSpec(memory_space=pltpu.VMEM)
        hbm = pl.BlockSpec(memory_space=pltpu.HBM)
        hops = len(doublings(n_row, n_col))
        n_sends = 6 + 2 * (nx // grp) + 2
        found = pl.pallas_call(
            functools.partial(kernel, n_row, n_col, grp),
            out_shape=(
                pltpu.VMEM((nx, ny, nz), F32),
                pltpu.VMEM((len(LEVELS), GROUPS), F32),
            ),
            in_specs=[hbm] * (3 + len(weights)),
            out_specs=(vmem, vmem),
            scratch_shapes=[
                pltpu.VMEM((nx, ny, nz), F32),
                pltpu.VMEM((nx, ny, nz), F32),
                pltpu.VMEM((nx + 6, ny, nz), F32),
                pltpu.VMEM((6, ny, nz), F32),
                pltpu.VMEM((6, ny, nz), F32),
                pltpu.VMEM((6, nx, nz), F32),
                pltpu.VMEM((6, nx, nz), F32),
                pltpu.VMEM((6, TILE, nz), F32),
                pltpu.VMEM((6, TILE, nz), F32),
                pltpu.VMEM((1, LANES), F32),
                pltpu.VMEM((devices, 1, LANES), F32),
                pltpu.SMEM(cut_exponent.shape, jnp.int32),
                pltpu.SMEM(group_map.shape, jnp.int32),
                *(pltpu.VMEM(w.shape, BF16) for w in weights),
                pltpu.SemaphoreType.DMA((nx // grp,)),
                pltpu.SemaphoreType.DMA((len(weights) + 2,)),
                pltpu.SemaphoreType.DMA((n_sends,)),
                pltpu.SemaphoreType.DMA((n_sends,)),
                pltpu.SemaphoreType.DMA((devices,)),
                pltpu.SemaphoreType.DMA((devices,)),
                pltpu.SemaphoreType.REGULAR((max(hops, 1),)),
            ],
            compiler_params=pltpu.CompilerParams(
                collective_id=0, has_side_effects=True, vmem_limit_bytes=24 * 2**20
            ),
        )(*(pltpu.with_memory_space_constraint(x, pltpu.HBM) for x in (cut_exponent, group_map, pressure, *weights)))
        coeffs, mass = pl.pallas_call(
            deliver,
            out_shape=tuple(pltpu.HBM(f.shape, F32) for f in found),
            in_specs=[vmem] * 2,
            out_specs=(hbm, hbm),
            scratch_shapes=[pltpu.SemaphoreType.DMA((8,)), pltpu.SemaphoreType.DMA],
            compiler_params=pltpu.CompilerParams(vmem_limit_bytes=2**20),
        )(*(pltpu.with_memory_space_constraint(x, pltpu.VMEM) for x in found))
        return coeffs, mass.T

    specs = P("row", "col", None)
    return jax.shard_map(
        shards, mesh=mesh, in_specs=(specs,) * 3, out_specs=(specs, P()), check_vma=False
    )
```

time: 29.2 us -> 26 us (0.89)
  Pallas kernels: 28.4 us -> 25.2 us
    pallas_call x2, Pallas kernels: 28.4 us -> 25.2 us  [the longest x1 23.8 us: shards(): pl.pallas_call(functools.partial(kernel, n_row, n_col, grp), out_shape=(p...]
where the time goes in v1:
time: 26 us; the launch traced here: 25.8 us
  Pallas kernels  25.2 us (97%)
  between operations  0.64 us (2%)
    pallas_call x1, Pallas kernels, shards(): pl.pallas_call(functools.partial(kernel, n_row, n_col, grp), out_shape=(p...  23.8 us
    pallas_call x1, Pallas kernels, shards(): pl.pallas_call(deliver, out_shape=tuple((pltpu.HBM(f.shape, F32) for f in...  1.39 us

profile of v1, /device:TPU:0, one launch (start us, length us, event | category | flops | bytes accessed | tf_op | source)
XLA Modules:
  0.0 25.8 jit_solution(16774151470909816323)
XLA Ops:
  0.6 23.8 %shard_map.122 = (f32[32,32,512]{2,1,0:T(8,128)S(1)}, f32[4,16]{1,0:T(4,128)S(1)}) custom-call(s32[1,1,2]{2,1,0:T(1,128)} %cut_hbm.1, s32[1,1,2]{2,1,0:T(1,128)} %map_hbm.1, f32[32,32,512]{2,1,0:T(8,128)} %p_ref.1, bf16[48,256]{1,0:T(8,128)(2,1)} %constant.16.clone.refs_0_, bf16[512,512]{1,0:T(8,128)(2,1)} %constant.17.clone.refs_1_, ...), custom_call_target="tpu_custom_call" | custom-call | tf_op jit(solution)/shard_map/pallas_call | solution.py:405
  24.4 1.4 %shard_map.123 = (f32[32,32,512]{2,1,0:T(8,128)}, f32[4,16]{1,0:T(4,128)}) custom-call(f32[32,32,512]{2,1,0:T(8,128)S(1)} %get-tuple-element.6.c_ref, f32[4,16]{1,0:T(4,128)S(1)} %get-tuple-element.7.m_ref), custom_call_target="tpu_custom_call" | custom-call | tf_op jit(solution)/shard_map/pallas_call | solution.py:440

commit v2 on v1

--- a/solution.py
+++ b/solution.py
@@ -71,6 +71,10 @@
     return dot(hi, right) + dot(lo, right)
 
 
+def dot_pair(left, right):
+    return jnp.dot(left, jnp.concatenate(split(right), 0), preferred_element_type=F32)
+
+
 def doublings(n_row, n_col):
     hops, known = [], 1
     while known < n_col // 2:
@@ -83,13 +87,40 @@
     return hops
 
 
+def band(first_row, coefs):
+    shape = (2 * TILE, LANES)
+    lane = lax.broadcasted_iota(jnp.int32, shape, 1)
+    far = jnp.abs(lane - lax.broadcasted_iota(jnp.int32, shape, 0) + first_row)
+    value = jnp.zeros(shape, F32)
+    for k, (even, odd) in enumerate(coefs):
+        if even or odd:
+            value = jnp.where(far == k, jnp.where(lane % 2 == 1, odd, even), value)
+    return value.astype(BF16)
+
+
+def fill_cyclic(ref):
+    n = ref.shape[0]
+    full = cyclic_matrix(n)
+    reach = 7
+    coefs = [(float(full[0, k]), float(full[1, 1 + k])) for k in range(reach)]
+    made = {}
+    for r in range(0, n, 2 * TILE):
+        for c in range(0, n, LANES):
+            off = (c - r + n // 2) % n - n // 2
+            near = off - 2 * TILE < reach and off + LANES > -reach
+            key = off if near else None
+            if key not in made:
+                made[key] = band(off, coefs) if near else jnp.zeros((2 * TILE, LANES), BF16)
+            ref[pl.ds(r, 2 * TILE), pl.ds(c, LANES)] = made[key]
+
+
 def kernel(n_row, n_col, grp, cut_hbm, map_hbm, p_ref, *refs):
-    weights, refs = refs[:8], refs[8:]
+    weights, refs = refs[:4], refs[4:]
     out_ref, mass_ref = refs[:2]
-    ext, v, q, hs, h, su, u, sc, cb, part, slots, cut_ref, map_ref = refs[2:15]
-    held = refs[15:23]
-    ws_ref, wz_ref, wy_ref, wu_ref, wsa_ref, wxa_ref, wxb_ref, wc_ref = held
-    in_sem, w_sem, h_send, h_recv, g_send, g_recv, hop_sem = refs[23:]
+    ext, q, hs, yh, sh, ch, su, u, part, slots, cut_ref, map_ref, wz_ref = refs[2:15]
+    held = refs[15:19]
+    wx_ref, wy_ref, wc_ref, wu_ref = held
+    in_sem, w_sem, h_send, h_recv, g_send, g_recv, hop_sem = refs[19:]
     nx, ny, nz = p_ref.shape
     half = nx // 2
     devices = n_row * n_col
@@ -104,20 +135,22 @@
         pl.semaphore_signal(barrier, inc=1, device_id=(r, c), device_id_type=MESH)
 
     loads = []
-    starts = [0, nx - grp, *range(grp, nx - grp, grp)]
-    for i, at in enumerate(starts):
-        load = pltpu.make_async_copy(
-            p_ref.at[pl.ds(at, grp)], ext.at[pl.ds(at, grp)], in_sem.at[i]
-        )
-        load.start()
-        loads.append(load)
-    fetched = []
-    for i, (src, dst) in enumerate(
-        zip((*weights, cut_hbm, map_hbm), (*held, cut_ref, map_ref), strict=True)
-    ):
-        fetch = pltpu.make_async_copy(src, dst, w_sem.at[i])
-        fetch.start()
-        fetched.append(fetch)
+
+    def load(at, size):
+        i = len(loads)
+        at = pl.ds(at, size)
+        loads.append(pltpu.make_async_copy(p_ref.at[at], ext.at[at], in_sem.at[i]))
+        loads[i].start()
+
+    fetched = [
+        pltpu.make_async_copy(src, dst, w_sem.at[i])
+        for i, (src, dst) in enumerate(
+            zip((*weights, cut_hbm, map_hbm), (*held, cut_ref, map_ref), strict=True)
+        )
+    ]
+    for at in (*range(nx - 6, nx), *range(5)):
+        load(at, 1)
+    fetched[0].start()
 
     hops = doublings(n_row, n_col)
 
@@ -132,80 +165,132 @@
 
     def relay(k):
         if k < len(hops):
-            pl.semaphore_wait(hop_sem.at[k], 2)
-            if k + 1 < len(hops):
-                call(k + 1)
+            with jax.named_scope(f"r{k}"):
+                pl.semaphore_wait(hop_sem.at[k], 2)
+                if k + 1 < len(hops):
+                    call(k + 1)
 
     sends = []
 
-    def send(src, dst, to):
-        i = len(sends)
-        copy = pltpu.make_async_remote_copy(
+    def remote(i, src, dst, to):
+        return pltpu.make_async_remote_copy(
             src_ref=src, dst_ref=dst, send_sem=h_send.at[i], recv_sem=h_recv.at[i],
             device_id=to, device_id_type=MESH,
         )
+
+    def send(src, dst, to):
+        copy = remote(len(sends), src, dst, to)
         copy.start()
         sends.append(copy)
         return copy
 
+    def halo(piece, way):
+        if isinstance(piece, int) and piece == 0:
+            rows = pl.ds(TILE, ny - 2 * TILE)
+        else:
+            rows = pl.ds(pl.multiple_of((piece - 1) * (ny - TILE), TILE), TILE)
+        three = lambda at: pl.ds(at + 3 * way, 3)
+        to = lax.rem(row + 1 + way * (n_row - 2), n_row)
+        return remote(
+            2 + 2 * piece + way, yh.at[three(0), rows], q.at[three(nx), rows], (to, col)
+        )
+
+    with jax.named_scope("wz"):
+        fill_cyclic(wz_ref)
+        sh[:, pl.ds(6, TILE - 6), :] = jnp.zeros((6, TILE - 6, nz), F32)
     with jax.named_scope("ld01"):
-        loads[0].wait()
-        loads[1].wait()
+        for copy in loads:
+            copy.wait()
+        fetched[0].wait()
+    edges = len(loads)
+    mid = nx - 11
+    third = mid // 3
+    for at in range(3):
+        load(5 + at * third, third if at < 2 else mid - 2 * third)
+    for fetch in fetched[1:]:
+        fetch.start()
     with jax.named_scope("hs"):
-        for i, plane in enumerate(partials_low(lambda i: ext[i], nx) + partials_high(lambda i: ext[i])):
+        planes = partials_low(lambda i: ext[i], nx) + partials_high(lambda i: ext[i])
+        for i, plane in enumerate(planes):
             hs[i] = plane
+            line = lambda j: plane[j : j + 1]
+            for k, one in enumerate(partials_low(line, ny) + partials_high(line)):
+                sh[k, pl.ds(i, 1), :] = one
+    lo, hi = pl.ds(0, 3), pl.ds(3, 3)
+    odd_core = lax.rem(col, 2)
+    is_last = (row == n_row - 1).astype(jnp.int32)
+    is_first = (row == 0).astype(jnp.int32)
+    far = is_first + (1 - is_first) * (1 - is_last) * odd_core
+    ways = (far + odd_core - 2 * far * odd_core, 1 - (far + odd_core - 2 * far * odd_core))
+    tail = (
+        (1, ways[0]), (2 - odd_core, far),
+        (1 + odd_core, odd_core * far + (1 - odd_core) * (1 - far)), (2, 1 - far),
+    )
+
+    outer_rows = (pl.ds(0, TILE), pl.ds(ny - TILE, TILE))
+
+    def lift(way):
+        three = pl.ds(3 * way, 3)
+        lifted = dot2(hs[three].reshape(3 * ny, nz), wz_ref[...])
+        yh[three] = dot_pair(wx_ref[...], lifted).reshape(3, ny, nz)
+
+    with jax.named_scope("lift0"):
+        lift(ways[0])
     with jax.named_scope("bar"):
         pl.semaphore_wait(barrier, 4)
-    lo, hi = pl.ds(0, 3), pl.ds(3, 3)
-    outer, inner = [], []
-    for rows, kept in (
-        (pl.ds(0, TILE), outer), (pl.ds(ny - TILE, TILE), outer),
-        (pl.ds(TILE, ny - 2 * TILE), inner),
-    ):
-        kept.append(send(hs.at[lo, rows], h.at[lo, rows], (up_r, col)))
-        kept.append(send(hs.at[hi, rows], h.at[hi, rows], (dn_r, col)))
+    corner = [
+        send(sh.at[lo], ch.at[lo], (row, up_c)),
+        send(sh.at[hi], ch.at[hi], (row, dn_c)),
+    ]
+    inner, *outer = [[halo(piece, way) for way in range(2)] for piece in range(3)]
+    sends.extend(inner + outer[0] + outer[1])
+    halo(0, ways[0]).start()
     if hops:
         call(0)
-
-    with jax.named_scope("su"):
-        fetched[0].wait()
-        near = []
-        for i, at in enumerate(starts):
-            if i > 1:
-                loads[i].wait()
-            at = pl.ds(at, grp)
-            got = dot2(ws_ref[...], ext[at].reshape(grp * ny, nz))
-            su[:, at, :] = got.reshape(6, grp, nz)
-            near.append(send(su.at[lo, at], u.at[lo, at], (row, up_c)))
-            near.append(send(su.at[hi, at], u.at[hi, at], (row, dn_c)))
+    with jax.named_scope("lift1"):
+        lift(ways[1])
+    halo(0, ways[1]).start()
+
+    groups = nx // grp
+    near = {}
+
+    def z_group(g):
+        at = pl.ds(g * grp, grp)
+        v = dot2(ext[at].reshape(grp * ny, nz), wz_ref[...])
+        got = dot2(wy_ref[...], v)
+        q[at] = got[: grp * ny].reshape(grp, ny, nz)
+        su[:, at, :] = got[grp * ny :].reshape(6, grp, nz)
+        near[g] = (
+            send(su.at[lo, at], u.at[lo, at], (row, up_c)),
+            send(su.at[hi, at], u.at[hi, at], (row, dn_c)),
+        )
+
+    with jax.named_scope("ld2"):
+        for copy in loads[edges:]:
+            copy.wait()
+        for fetch in fetched[1:]:
+            fetch.wait()
+    order = (0, groups - 1, *range(1, groups - 1))
+    with jax.named_scope("z"):
+        for g in order[: groups // 2]:
+            z_group(g)
     relay(0)
-    groups = nx // grp
-    with jax.named_scope("z"):
-        fetched[1].wait()
-        for g in range(groups):
-            at = pl.ds(g * grp, grp)
-            v[at] = dot2(ext[at].reshape(grp * ny, nz), wz_ref[...]).reshape(grp, ny, nz)
-            if g == groups // 2 - 1:
-                relay(1)
-    relay(2)
-    with jax.named_scope("y"):
-        for fetch in fetched[2:]:
-            fetch.wait()
-        for g in range(groups):
-            at = pl.ds(g * grp, grp)
-            q[at] = dot2(wy_ref[...], v[at].reshape(grp * ny, nz)).reshape(grp, ny, nz)
-    relay(3)
-    with jax.named_scope("wait_u"):
-        for copy in near:
+    with jax.named_scope("z2"):
+        z_group(order[groups // 2])
+    with jax.named_scope("wait_corner"):
+        for copy in corner:
             copy.wait_recv()
-    with jax.named_scope("u"):
-        zu = dot2(u[...].reshape(6 * nx, nz), wz_ref[...]).reshape(6, nx, nz)
-        for g in range(groups):
-            at = slice(g * grp, (g + 1) * grp)
-            more = dot2(wu_ref[...], zu[:, at, :].reshape(6 * grp, nz))
-            q[at] += more.reshape(grp, ny, nz)
-    for k in range(4, len(hops)):
-        relay(k)
+    with jax.named_scope("outer"):
+        lifted = dot2(ch[...].reshape(6 * TILE, nz), wz_ref[...])
+        more = dot_pair(wc_ref[...], lifted).reshape(6, 2 * TILE, nz)
+        for k, rows in enumerate(outer_rows):
+            yh[:, rows, :] += more[:, k * TILE : (k + 1) * TILE, :]
+        for piece, way in tail:
+            halo(piece, way).start()
+    with jax.named_scope("z3"):
+        for g in order[groups // 2 + 1 :]:
+            z_group(g)
+    relay(1)
 
     zb = cut_ref.shape[2]
     width = nz // zb
@@ -213,7 +298,7 @@
     odd = lambda axis: lax.broadcasted_iota(jnp.int32, (TILE, LANES), axis) % 2
     mixed = (odd(0) + odd(1)) > 0
 
-    def x_stage(totals, edges):
+    def x_stage(totals, edges, first, last):
         totals = list(totals)
         for z in range(zb):
             cuts = jnp.full((TILE, LANES), -cut_ref[0, 0, z], jnp.int32)
@@ -271,37 +356,40 @@
                 return tuple(sums)
 
             mine = slice(z * n_lev, (z + 1) * n_lev)
-            totals[mine] = lax.fori_loop(0, ny // TILE, tile, tuple(totals[mine]))
+            totals[mine] = lax.fori_loop(first, last, tile, tuple(totals[mine]))
         return totals
 
-    with jax.named_scope("wait_outer"):
-        for copy in outer:
-            copy.wait_recv()
-    with jax.named_scope("corner"):
-        rim = jnp.concatenate([h[:, :TILE, :], h[:, ny - TILE :, :]], 1).reshape(12 * TILE, nz)
-        zrim = dot2(rim, wz_ref[...])
-        sc[...] = dot2(wsa_ref[...], zrim).reshape(6, TILE, nz)
-        corner = [
-            send(sc.at[lo], cb.at[lo], (row, up_c)),
-            send(sc.at[hi], cb.at[hi], (row, dn_c)),
-        ]
-        q[pl.ds(nx, 6)] = dot2(wxa_ref[...], zrim).reshape(6, ny, nz)
+    tiles = ny // TILE
+    totals = [jnp.zeros((TILE, LANES), F32) for _ in range(zb * n_lev)]
     with jax.named_scope("xin"):
-        totals = [jnp.zeros((TILE, LANES), F32) for _ in range(zb * n_lev)]
-        totals = x_stage(totals, False)
+        totals = x_stage(totals, False, 1, tiles - 1)
+    relay(2)
     with jax.named_scope("wait_inner"):
         for copy in inner:
             copy.wait_recv()
-    with jax.named_scope("wait_corner"):
-        for copy in corner:
-            copy.wait_recv()
-    with jax.named_scope("edge"):
-        core = h[:, TILE : ny - TILE, :].reshape(6 * (ny - 2 * TILE), nz)
-        edge = dot2(wxb_ref[...], dot2(core, wz_ref[...]))
-        edge += dot2(wc_ref[...], cb[...].reshape(6 * TILE, nz))
-        q[pl.ds(nx, 6)] += edge.reshape(6, ny, nz)
-    with jax.named_scope("xedge"):
-        totals = x_stage(totals, True)
+    with jax.named_scope("xinner"):
+        totals = x_stage(totals, True, 1, tiles - 1)
+    for g in order:
+        with jax.named_scope("wait_u"):
+            for copy in near[g]:
+                copy.wait_recv()
+        with jax.named_scope("u"):
+            at = pl.ds(g * grp, grp)
+            more = dot_pair(wu_ref[...], u[:, at, :].reshape(6 * grp, nz))
+            more = more.reshape(grp, 2 * TILE, nz)
+            for k, rows in enumerate(outer_rows):
+                q[at, rows, :] += more[:, k * TILE : (k + 1) * TILE, :]
+    for k in range(3, len(hops)):
+        relay(k)
+    with jax.named_scope("xin2"):
+        for t in (0, tiles - 1):
+            totals = x_stage(totals, False, t, t + 1)
+    for k, t in enumerate((0, tiles - 1)):
+        with jax.named_scope("wait_outer"):
+            for copy in outer[k]:
+                copy.wait_recv()
+        with jax.named_scope("xouter"):
+            totals = x_stage(totals, True, t, t + 1)
     with jax.named_scope("line"):
         lane = lax.broadcasted_iota(jnp.int32, (1, LANES), 1)
         line = jnp.zeros((1, LANES), F32)
@@ -382,26 +470,22 @@
         devices = n_row * n_col
         local = local_matrix(ny)
         own, beyond = local[:, :ny], local[:, ny:]
-        wy = np.kron(np.eye(grp), own)
-        wu = np.einsum("xw,yk->xykw", np.eye(grp), beyond).reshape(grp * ny, 6 * grp)
         eye = np.eye(ny)
         take = lambda i: eye[i]
         near = np.stack(partials_low(take, ny) + partials_high(take))
         ws = np.einsum("ky,xw->kxwy", near, np.eye(grp)).reshape(6 * grp, grp * ny)
+        wy = np.concatenate([np.kron(np.eye(grp), own), ws])
         rim = np.r_[0:TILE, ny - TILE : ny]
-        six = np.eye(6, TILE).T
-        wsa = np.einsum("ky,wp->kwpy", near[:, rim], six).reshape(6 * TILE, 6 * 2 * TILE)
-        wxa = np.kron(np.eye(6), own[:, rim])
-        wxb = np.kron(np.eye(6), own[:, TILE : ny - TILE])
-        wc = np.einsum("wp,yk->pykw", six, beyond).reshape(6 * ny, 6 * TILE)
-        weights = [
-            jnp.asarray(w, BF16)
-            for w in (ws, cyclic_matrix(nz).T, wy, wu, wsa, wxa, wxb, wc)
-        ]
+        spread = lambda planes: np.einsum("wp,yk->pykw", planes, beyond[rim]).reshape(
+            planes.shape[1] * 2 * TILE, -1
+        )
+        wx, wc, wu = np.kron(np.eye(3), own), spread(np.eye(TILE, 6)), spread(np.eye(grp))
+        twice = lambda w: np.tile(w, 2)
+        weights = [jnp.asarray(w, BF16) for w in (twice(wx), wy, twice(wc), twice(wu))]
         vmem = pl.BlockSpec(memory_space=pltpu.VMEM)
         hbm = pl.BlockSpec(memory_space=pltpu.HBM)
         hops = len(doublings(n_row, n_col))
-        n_sends = 6 + 2 * (nx // grp) + 2
+        n_sends = 8 + 2 * (nx // grp)
         found = pl.pallas_call(
             functools.partial(kernel, n_row, n_col, grp),
             out_shape=(
@@ -412,20 +496,20 @@
             out_specs=(vmem, vmem),
             scratch_shapes=[
                 pltpu.VMEM((nx, ny, nz), F32),
-                pltpu.VMEM((nx, ny, nz), F32),
                 pltpu.VMEM((nx + 6, ny, nz), F32),
                 pltpu.VMEM((6, ny, nz), F32),
                 pltpu.VMEM((6, ny, nz), F32),
+                pltpu.VMEM((6, TILE, nz), F32),
+                pltpu.VMEM((6, TILE, nz), F32),
                 pltpu.VMEM((6, nx, nz), F32),
                 pltpu.VMEM((6, nx, nz), F32),
-                pltpu.VMEM((6, TILE, nz), F32),
-                pltpu.VMEM((6, TILE, nz), F32),
                 pltpu.VMEM((1, LANES), F32),
                 pltpu.VMEM((devices, 1, LANES), F32),
                 pltpu.SMEM(cut_exponent.shape, jnp.int32),
                 pltpu.SMEM(group_map.shape, jnp.int32),
+                pltpu.VMEM((nz, nz), BF16),
                 *(pltpu.VMEM(w.shape, BF16) for w in weights),
-                pltpu.SemaphoreType.DMA((nx // grp,)),
+                pltpu.SemaphoreType.DMA((14,)),
                 pltpu.SemaphoreType.DMA((len(weights) + 2,)),
                 pltpu.SemaphoreType.DMA((n_sends,)),
                 pltpu.SemaphoreType.DMA((n_sends,)),

time: 26 us -> 24 us (0.923)
  Pallas kernels: 25.2 us -> 23.1 us
    pallas_call x1, Pallas kernels: 23.8 us -> 21.8 us  [shards(): pl.pallas_call(functools.partial(kernel, n_row, n_col, grp), out_shape=(p...]
where the time goes in v2:
time: 24 us; the launch traced here: 23.8 us
  Pallas kernels  23.1 us (96%)
  between operations  0.64 us (3%)
    pallas_call x1, Pallas kernels, shards(): pl.pallas_call(functools.partial(kernel, n_row, n_col, grp), out_shape=(p...  21.8 us
    pallas_call x1, Pallas kernels, shards(): pl.pallas_call(deliver, out_shape=tuple((pltpu.HBM(f.shape, F32) for f in...  1.39 us

profile of v2, /device:TPU:0, one launch (start us, length us, event | category | flops | bytes accessed | tf_op | source)
XLA Modules:
  0.0 23.8 jit_solution(2157420463811930092)
XLA Ops:
  0.6 21.8 %shard_map.86 = (f32[32,32,512]{2,1,0:T(8,128)S(1)}, f32[4,16]{1,0:T(4,128)S(1)}) custom-call(s32[1,1,2]{2,1,0:T(1,128)} %cut_hbm.1, s32[1,1,2]{2,1,0:T(1,128)} %map_hbm.1, f32[32,32,512]{2,1,0:T(8,128)} %p_ref.1, bf16[96,192]{1,0:T(8,128)(2,1)} %constant.8.clone.refs_0_, bf16[304,256]{1,0:T(8,128)(2,1)} %constant.9.clone.refs_1_, ...), custom_call_target="tpu_custom_call" | custom-call | tf_op jit(solution)/shard_map/pallas_call | solution.py:489
  22.4 1.4 %shard_map.87 = (f32[32,32,512]{2,1,0:T(8,128)}, f32[4,16]{1,0:T(4,128)}) custom-call(f32[32,32,512]{2,1,0:T(8,128)S(1)} %get-tuple-element.6.c_ref, f32[4,16]{1,0:T(4,128)S(1)} %get-tuple-element.7.m_ref), custom_call_target="tpu_custom_call" | custom-call | tf_op jit(solution)/shard_map/pallas_call | solution.py:524

commit v3 on v2

--- a/solution.py
+++ b/solution.py
@@ -120,7 +120,7 @@
     ext, q, hs, yh, sh, ch, su, u, part, slots, cut_ref, map_ref, wz_ref = refs[2:15]
     held = refs[15:19]
     wx_ref, wy_ref, wc_ref, wu_ref = held
-    in_sem, w_sem, h_send, h_recv, g_send, g_recv, hop_sem = refs[19:]
+    in_sem, w_sem, h_send, h_recv, g_send, g_recv, hop_sem, last_sem = refs[19:]
     nx, ny, nz = p_ref.shape
     half = nx // 2
     devices = n_row * n_col
@@ -131,16 +131,15 @@
     up_r, dn_r, up_c, dn_c = away_r(1), away_r(-1), away_c(1), away_c(-1)
 
     barrier = pltpu.get_barrier_semaphore()
-    for r, c in ((up_r, col), (dn_r, col), (row, up_c), (row, dn_c)):
-        pl.semaphore_signal(barrier, inc=1, device_id=(r, c), device_id_type=MESH)
-
-    loads = []
-
-    def load(at, size):
-        i = len(loads)
-        at = pl.ds(at, size)
-        loads.append(pltpu.make_async_copy(p_ref.at[at], ext.at[at], in_sem.at[i]))
-        loads[i].start()
+    top = n_row - 1
+    at_first, at_last = row == 0, row == top
+
+    def signal(sem, r, c):
+        pl.semaphore_signal(sem, inc=1, device_id=(r, c), device_id_type=MESH)
+
+    for r, c in ((dn_r, col), (row, up_c), (row, dn_c)):
+        signal(barrier, r, c)
+    pl.when(jnp.logical_not(at_last))(lambda: signal(barrier, row + 1, col))
 
     fetched = [
         pltpu.make_async_copy(src, dst, w_sem.at[i])
@@ -148,8 +147,23 @@
             zip((*weights, cut_hbm, map_hbm), (*held, cut_ref, map_ref), strict=True)
         )
     ]
-    for at in (*range(nx - 6, nx), *range(5)):
-        load(at, 1)
+    odd_core = lax.rem(col, 2)
+
+    def first_way(r):
+        return lax.select(r == 0, 0, lax.select(r == top, odd_core, 1 - odd_core))
+
+    ways = (first_way(row), 1 - first_way(row))
+    needs = ((nx - 2, nx - 1, nx - 4, nx - 3, nx - 6), (0, 2, 1, 4))
+    rest = sorted(set(range(nx)) - set(sum(needs, ())))
+
+    def planes_of(way, act):
+        for k, plane in enumerate(needs[way]):
+            at = pl.ds(plane, 1)
+            act(pltpu.make_async_copy(p_ref.at[at], ext.at[at], in_sem.at[5 * way + k]))
+
+    for flip in range(2):
+        for way in range(2):
+            pl.when(ways[flip] == way)(lambda: planes_of(way, lambda copy: copy.start()))
     fetched[0].start()
 
     hops = doublings(n_row, n_col)
@@ -161,7 +175,7 @@
         else:
             aim = ((away_r(far), col), (away_r(-far), col))
         for to in aim:
-            pl.semaphore_signal(hop_sem.at[k], inc=1, device_id=to, device_id_type=MESH)
+            signal(hop_sem.at[k], *to)
 
     def relay(k):
         if k < len(hops):
@@ -198,59 +212,86 @@
     with jax.named_scope("wz"):
         fill_cyclic(wz_ref)
         sh[:, pl.ds(6, TILE - 6), :] = jnp.zeros((6, TILE - 6, nz), F32)
-    with jax.named_scope("ld01"):
-        for copy in loads:
-            copy.wait()
+    def call_first():
+        pl.semaphore_wait(barrier, 4)
+        signal(last_sem, 0, col)
+
+    with jax.named_scope("barl"):
+        pl.when(at_last)(call_first)
+
+    def prepare(way):
+        planes_of(way, lambda copy: copy.wait())
+        made = (partials_low, partials_high)[way]
+        planes = made(lambda i: ext[i], *((nx,) if way == 0 else ()))
+        for i, plane in enumerate(planes):
+            hs[3 * way + i] = plane
+
+    with jax.named_scope("hs0"):
+        for way in range(2):
+            pl.when(ways[0] == way)(lambda: prepare(way))
         fetched[0].wait()
-    edges = len(loads)
-    mid = nx - 11
-    third = mid // 3
-    for at in range(3):
-        load(5 + at * third, third if at < 2 else mid - 2 * third)
-    for fetch in fetched[1:]:
-        fetch.start()
-    with jax.named_scope("hs"):
-        planes = partials_low(lambda i: ext[i], nx) + partials_high(lambda i: ext[i])
-        for i, plane in enumerate(planes):
-            hs[i] = plane
-            line = lambda j: plane[j : j + 1]
+    inside = 3 * (ny - 2 * TILE)
+    inner_rows = pl.ds(TILE, ny - 2 * TILE)
+    outer_rows = (pl.ds(0, TILE), pl.ds(ny - TILE, TILE))
+    plane_rows = lambda way: hs[pl.ds(3 * way, 3)].reshape(3 * ny, nz)
+
+    def lift_inner(way, data):
+        made = dot_pair(wx_ref[pl.ds(0, inside)], data)
+        yh[pl.ds(3 * way, 3), inner_rows, :] = made.reshape(3, ny - 2 * TILE, nz)
+
+    def lift_outer(way, data):
+        made = dot_pair(wx_ref[pl.ds(inside, 6 * TILE)], data).reshape(3, 2 * TILE, nz)
+        for k, rows in enumerate(outer_rows):
+            yh[pl.ds(3 * way, 3), rows, :] = made[:, k * TILE : (k + 1) * TILE, :]
+
+    with jax.named_scope("lift0"):
+        lift_inner(ways[0], plane_rows(ways[0]))
+    with jax.named_scope("bar"):
+        pl.when(at_first)(lambda: pl.semaphore_wait(barrier, 3))
+        pl.when(jnp.logical_not(at_first | at_last))(lambda: pl.semaphore_wait(barrier, 4))
+    halo(0, ways[0]).start()
+    with jax.named_scope("hs1"):
+        for way in range(2):
+            pl.when(ways[1] == way)(lambda: prepare(way))
+        for i in range(6):
+            line = lambda j: hs[i, pl.ds(j, 1), :]
             for k, one in enumerate(partials_low(line, ny) + partials_high(line)):
                 sh[k, pl.ds(i, 1), :] = one
     lo, hi = pl.ds(0, 3), pl.ds(3, 3)
-    odd_core = lax.rem(col, 2)
-    is_last = (row == n_row - 1).astype(jnp.int32)
-    is_first = (row == 0).astype(jnp.int32)
-    far = is_first + (1 - is_first) * (1 - is_last) * odd_core
-    ways = (far + odd_core - 2 * far * odd_core, 1 - (far + odd_core - 2 * far * odd_core))
-    tail = (
-        (1, ways[0]), (2 - odd_core, far),
-        (1 + odd_core, odd_core * far + (1 - odd_core) * (1 - far)), (2, 1 - far),
-    )
-
-    outer_rows = (pl.ds(0, TILE), pl.ds(ny - TILE, TILE))
-
-    def lift(way):
-        three = pl.ds(3 * way, 3)
-        lifted = dot2(hs[three].reshape(3 * ny, nz), wz_ref[...])
-        yh[three] = dot_pair(wx_ref[...], lifted).reshape(3, ny, nz)
-
-    with jax.named_scope("lift0"):
-        lift(ways[0])
-    with jax.named_scope("bar"):
-        pl.semaphore_wait(barrier, 4)
     corner = [
         send(sh.at[lo], ch.at[lo], (row, up_c)),
         send(sh.at[hi], ch.at[hi], (row, dn_c)),
     ]
     inner, *outer = [[halo(piece, way) for way in range(2)] for piece in range(3)]
     sends.extend(inner + outer[0] + outer[1])
-    halo(0, ways[0]).start()
     if hops:
         call(0)
+    loads = []
+    for i in range(3):
+        at = pl.ds(5 + i * ((nx - 11) // 3), (nx - 11) // 3)
+        if i == 2:
+            at = pl.ds(5 + 2 * ((nx - 11) // 3), nx - 11 - 2 * ((nx - 11) // 3))
+        loads.append(pltpu.make_async_copy(p_ref.at[at], ext.at[at], in_sem.at[10 + i]))
+    for i, plane in enumerate((3, nx - 5)):
+        at = pl.ds(plane, 1)
+        loads.append(pltpu.make_async_copy(p_ref.at[at], ext.at[at], in_sem.at[13 + i]))
+    for copy in loads:
+        copy.start()
+    for fetch in fetched[1:]:
+        fetch.start()
     with jax.named_scope("lift1"):
-        lift(ways[1])
-    halo(0, ways[1]).start()
-
+        lifted = dot2(plane_rows(ways[1]), wz_ref[...])
+        lift_inner(ways[1], lifted)
+    pl.when(jnp.logical_not(at_first))(lambda: halo(0, ways[1]).start())
+    with jax.named_scope("lift2"):
+        lift_outer(ways[1], lifted)
+        lift_outer(ways[0], dot2(plane_rows(ways[0]), wz_ref[...]))
+
+    far = lax.select(at_first, 1, lax.select(at_last, 0, odd_core))
+    tail = (
+        (1, far + odd_core - 2 * far * odd_core), (2 - odd_core, far),
+        (1 + odd_core, odd_core * far + (1 - odd_core) * (1 - far)), (2, 1 - far),
+    )
     groups = nx // grp
     near = {}
 
@@ -266,7 +307,7 @@
         )
 
     with jax.named_scope("ld2"):
-        for copy in loads[edges:]:
+        for copy in loads:
             copy.wait()
         for fetch in fetched[1:]:
             fetch.wait()
@@ -274,6 +315,13 @@
     with jax.named_scope("z"):
         for g in order[: groups // 2]:
             z_group(g)
+    with jax.named_scope("last"):
+
+        @pl.when(at_first)
+        def _():
+            pl.semaphore_wait(last_sem, 1)
+            halo(0, ways[1]).start()
+
     relay(0)
     with jax.named_scope("z2"):
         z_group(order[groups // 2])
@@ -367,6 +415,14 @@
     with jax.named_scope("wait_inner"):
         for copy in inner:
             copy.wait_recv()
+
+        def make_up(way):
+            at = pl.ds(nx + 3 * way, 3)
+            raw = q[at, inner_rows, :].reshape(inside, nz)
+            q[at, inner_rows, :] = dot2(raw, wz_ref[...]).reshape(3, ny - 2 * TILE, nz)
+
+        pl.when(first_way(dn_r) == 0)(lambda: make_up(0))
+        pl.when(first_way(up_r) == 1)(lambda: make_up(1))
     with jax.named_scope("xinner"):
         totals = x_stage(totals, True, 1, tiles - 1)
     for g in order:
@@ -391,13 +447,15 @@
         with jax.named_scope("xouter"):
             totals = x_stage(totals, True, t, t + 1)
     with jax.named_scope("line"):
-        lane = lax.broadcasted_iota(jnp.int32, (1, LANES), 1)
-        line = jnp.zeros((1, LANES), F32)
-        cells = nx * ny * width
-        for z in range(zb):
-            for n in range(n_lev):
-                mass = jnp.sum(totals[z * n_lev + n], keepdims=True) / cells
-                line += jnp.where(lane == n * GROUPS + map_ref[0, 0, z], mass, 0.0)
+        rows = zb * n_lev
+        lane, at = (lax.broadcasted_iota(jnp.int32, (rows, LANES), axis) for axis in (1, 0))
+        group = jnp.full((rows, LANES), map_ref[0, 0, 0], jnp.int32)
+        for z in range(1, zb):
+            group = jnp.where(at >= z * n_lev, map_ref[0, 0, z], group)
+        sums = jnp.concatenate([jnp.sum(total, axis=0, keepdims=True) for total in totals], 0)
+        mass = jnp.sum(sums, axis=1, keepdims=True) / (nx * ny * width)
+        line = jnp.where(lane == at % n_lev * GROUPS + group, mass, 0.0)
+        line = jnp.sum(line, axis=0, keepdims=True)
         part[...] = line
         slots[me] = line
 
@@ -415,7 +473,7 @@
 
     def peers(visit):
         if devices <= UNROLL:
-            for j in reversed(range(n_row)):
+            for j in (*range(1, n_row), 0):
                 for k in range(n_col):
                     if j or k:
                         r, c = away_r(j), away_c(k)
@@ -441,22 +499,23 @@
             copy.wait_send()
     with jax.named_scope("gather"):
         peers(lambda r, c, t: gather(r, c, t).wait())
-    with jax.named_scope("sum"):
-        total = jnp.sum(slots[...], axis=0)
-        mass_ref[...] = jnp.concatenate(
-            [total[:, n * GROUPS : (n + 1) * GROUPS] for n in range(n_lev)], 0
-        )
-
-
-def deliver(c_ref, m_ref, out_hbm, mass_hbm, sems, m_sem):
+    mass_ref[...] = slots[...]
+
+
+def deliver(c_ref, m_ref, out_hbm, mass_hbm, mass, sems, m_sem):
     count = sems.shape[0]
     size = c_ref.shape[0] // count
-    copies = [pltpu.make_async_copy(m_ref, mass_hbm, m_sem)]
+    copies = []
     for i in range(count):
         at = pl.ds(i * size, size)
         copies.append(pltpu.make_async_copy(c_ref.at[at], out_hbm.at[at], sems.at[i]))
-    for copy in copies:
-        copy.start()
+        copies[i].start()
+    total = jnp.sum(m_ref[...], axis=0)
+    mass[...] = jnp.concatenate(
+        [total[:, n * GROUPS : (n + 1) * GROUPS] for n in range(len(LEVELS))], 0
+    )
+    copies.append(pltpu.make_async_copy(mass, mass_hbm, m_sem))
+    copies[-1].start()
     for copy in copies:
         copy.wait()
 
@@ -479,7 +538,9 @@
         spread = lambda planes: np.einsum("wp,yk->pykw", planes, beyond[rim]).reshape(
             planes.shape[1] * 2 * TILE, -1
         )
-        wx, wc, wu = np.kron(np.eye(3), own), spread(np.eye(TILE, 6)), spread(np.eye(grp))
+        core = np.r_[TILE : ny - TILE]
+        wx = np.concatenate([np.kron(np.eye(3), own[rows]) for rows in (core, rim)])
+        wc, wu = spread(np.eye(TILE, 6)), spread(np.eye(grp))
         twice = lambda w: np.tile(w, 2)
         weights = [jnp.asarray(w, BF16) for w in (twice(wx), wy, twice(wc), twice(wu))]
         vmem = pl.BlockSpec(memory_space=pltpu.VMEM)
@@ -490,7 +551,7 @@
             functools.partial(kernel, n_row, n_col, grp),
             out_shape=(
                 pltpu.VMEM((nx, ny, nz), F32),
-                pltpu.VMEM((len(LEVELS), GROUPS), F32),
+                pltpu.VMEM((devices, 1, LANES), F32),
             ),
             in_specs=[hbm] * (3 + len(weights)),
             out_specs=(vmem, vmem),
@@ -509,13 +570,14 @@
                 pltpu.SMEM(group_map.shape, jnp.int32),
                 pltpu.VMEM((nz, nz), BF16),
                 *(pltpu.VMEM(w.shape, BF16) for w in weights),
-                pltpu.SemaphoreType.DMA((14,)),
+                pltpu.SemaphoreType.DMA((15,)),
                 pltpu.SemaphoreType.DMA((len(weights) + 2,)),
                 pltpu.SemaphoreType.DMA((n_sends,)),
                 pltpu.SemaphoreType.DMA((n_sends,)),
                 pltpu.SemaphoreType.DMA((devices,)),
                 pltpu.SemaphoreType.DMA((devices,)),
                 pltpu.SemaphoreType.REGULAR((max(hops, 1),)),
+                pltpu.SemaphoreType.REGULAR,
             ],
             compiler_params=pltpu.CompilerParams(
                 collective_id=0, has_side_effects=True, vmem_limit_bytes=24 * 2**20
@@ -523,10 +585,16 @@
         )(*(pltpu.with_memory_space_constraint(x, pltpu.HBM) for x in (cut_exponent, group_map, pressure, *weights)))
         coeffs, mass = pl.pallas_call(
             deliver,
-            out_shape=tuple(pltpu.HBM(f.shape, F32) for f in found),
+            out_shape=(
+                pltpu.HBM((nx, ny, nz), F32), pltpu.HBM((len(LEVELS), GROUPS), F32),
+            ),
             in_specs=[vmem] * 2,
             out_specs=(hbm, hbm),
-            scratch_shapes=[pltpu.SemaphoreType.DMA((8,)), pltpu.SemaphoreType.DMA],
+            scratch_shapes=[
+                pltpu.VMEM((len(LEVELS), GROUPS), F32),
+                pltpu.SemaphoreType.DMA((2,)),
+                pltpu.SemaphoreType.DMA,
+            ],
             compiler_params=pltpu.CompilerParams(vmem_limit_bytes=2**20),
         )(*(pltpu.with_memory_space_constraint(x, pltpu.VMEM) for x in found))
         return coeffs, mass.T

time: 24 us -> 23.7 us (0.987)
  no operation moved by 1% of the time
where the time goes in v3:
time: 23.7 us; the launch traced here: 23.5 us
  Pallas kernels  22.9 us (97%)
  between operations  0.64 us (3%)
    pallas_call x1, Pallas kernels, shards(): pl.pallas_call(functools.partial(kernel, n_row, n_col, grp), out_shape=(p...  21.5 us
    pallas_call x1, Pallas kernels, shards(): pl.pallas_call(deliver, out_shape=(pltpu.HBM((nx, ny, nz), F32), pltpu.HB...  1.35 us

profile of v3, /device:TPU:0, one launch (start us, length us, event | category | flops | bytes accessed | tf_op | source)
XLA Modules:
  0.0 23.5 jit_solution(17658156137101048024)
XLA Ops:
  0.6 21.5 %shard_map.86 = (f32[32,32,512]{2,1,0:T(8,128)S(1)}, f32[32,1,128]{2,1,0:T(1,128)S(1)}) custom-call(s32[1,1,2]{2,1,0:T(1,128)} %cut_hbm.1, s32[1,1,2]{2,1,0:T(1,128)} %map_hbm.1, f32[32,32,512]{2,1,0:T(8,128)} %p_ref.1, bf16[96,192]{1,0:T(8,128)(2,1)} %constant.8.clone.refs_0_, bf16[304,256]{1,0:T(8,128)(2,1)} %constant.9.clone.refs_1_, ...), custom_call_target="tpu_custom_call" | custom-call | tf_op jit(solution)/shard_map/pallas_call | solution.py:550
  22.2 1.4 %shard_map.87 = (f32[32,32,512]{2,1,0:T(8,128)}, f32[4,16]{1,0:T(4,128)}) custom-call(f32[32,32,512]{2,1,0:T(8,128)S(1)} %get-tuple-element.6.c_ref, f32[32,1,128]{2,1,0:T(1,128)S(1)} %get-tuple-element.7.m_ref), custom_call_target="tpu_custom_call" | custom-call | tf_op jit(solution)/shard_map/pallas_call | solution.py:586

commit v4 on v3

--- a/solution.py
+++ b/solution.py
@@ -98,11 +98,25 @@
     return value.astype(BF16)
 
 
+def inner_twice(n):
+    shape = (n - 2 * TILE, 2 * n)
+    row, cell = (lax.broadcasted_iota(jnp.int32, shape, axis) for axis in (0, 1))
+    far = jnp.abs(cell % n - row - TILE)
+    value = jnp.zeros(shape, F32)
+    for k, (even, odd) in enumerate(coefficients(n)):
+        value = jnp.where(far == k, jnp.where(row % 2 == 1, odd, even), value)
+    return value.astype(BF16)
+
+
+def coefficients(n):
+    full = cyclic_matrix(n)
+    return [(float(full[0, k]), float(full[1, 1 + k])) for k in range(7)]
+
+
 def fill_cyclic(ref):
     n = ref.shape[0]
-    full = cyclic_matrix(n)
-    reach = 7
-    coefs = [(float(full[0, k]), float(full[1, 1 + k])) for k in range(reach)]
+    coefs = coefficients(n)
+    reach = len(coefs)
     made = {}
     for r in range(0, n, 2 * TILE):
         for c in range(0, n, LANES):
@@ -115,14 +129,18 @@
 
 
 def kernel(n_row, n_col, grp, cut_hbm, map_hbm, p_ref, *refs):
-    weights, refs = refs[:4], refs[4:]
+    weights, refs = refs[:2], refs[2:]
     out_ref, mass_ref = refs[:2]
     ext, q, hs, yh, sh, ch, su, u, part, slots, cut_ref, map_ref, wz_ref = refs[2:15]
-    held = refs[15:19]
-    wx_ref, wy_ref, wc_ref, wu_ref = held
-    in_sem, w_sem, h_send, h_recv, g_send, g_recv, hop_sem, last_sem = refs[19:]
+    held = refs[15:17]
+    wx_ref, wall_ref = held
+    in_sem, w_sem, h_send, h_recv, g_sem, hop_sem, last_sem = refs[17:]
     nx, ny, nz = p_ref.shape
     half = nx // 2
+    tall = grp * ny + 6 * grp
+    wy_ref = wall_ref.at[pl.ds(0, tall)]
+    wc_ref = wall_ref.at[pl.ds(tall, 12 * TILE), pl.ds(0, 12 * TILE)]
+    wu_ref = wall_ref.at[pl.ds(tall + 12 * TILE, 2 * TILE * grp), pl.ds(0, 12 * grp)]
     devices = n_row * n_col
     row, col = lax.axis_index("row"), lax.axis_index("col")
     me = row * n_col + col
@@ -136,10 +154,6 @@
 
     def signal(sem, r, c):
         pl.semaphore_signal(sem, inc=1, device_id=(r, c), device_id_type=MESH)
-
-    for r, c in ((dn_r, col), (row, up_c), (row, dn_c)):
-        signal(barrier, r, c)
-    pl.when(jnp.logical_not(at_last))(lambda: signal(barrier, row + 1, col))
 
     fetched = [
         pltpu.make_async_copy(src, dst, w_sem.at[i])
@@ -154,17 +168,38 @@
 
     ways = (first_way(row), 1 - first_way(row))
     needs = ((nx - 2, nx - 1, nx - 4, nx - 3, nx - 6), (0, 2, 1, 4))
-    rest = sorted(set(range(nx)) - set(sum(needs, ())))
-
-    def planes_of(way, act):
-        for k, plane in enumerate(needs[way]):
-            at = pl.ds(plane, 1)
-            act(pltpu.make_async_copy(p_ref.at[at], ext.at[at], in_sem.at[5 * way + k]))
-
+
+    def take(at, i):
+        return pltpu.make_async_copy(p_ref.at[at], ext.at[at], in_sem.at[i])
+
+    def landed(ref, sem):
+        pltpu.make_async_copy(ref, ref, sem).wait()
+
+    head = lax.select(ways[0] == 0, needs[0][0], needs[1][0])
+    head_copy = take(pl.ds(head, 1), 0)
+    head_copy.start()
+    fetched[0].start()
     for flip in range(2):
         for way in range(2):
-            pl.when(ways[flip] == way)(lambda: planes_of(way, lambda copy: copy.start()))
-    fetched[0].start()
+
+            @pl.when(ways[flip] == way)
+            def _():
+                for plane in needs[way][1 - flip :]:
+                    take(pl.ds(plane, 1), 1 + flip).start()
+
+    loads = []
+    mid = nx - 11
+    starts = (5, 5 + mid // 3, 5 + 2 * (mid // 3), nx - 6)
+    for at, end in (*zip(starts[:-1], starts[1:], strict=True), (3, 4), (nx - 5, nx - 4)):
+        loads.append(take(pl.ds(at, end - at), 3))
+    for copy in loads:
+        copy.start()
+    for fetch in fetched[1:]:
+        fetch.start()
+
+    for r, c in ((dn_r, col), (row, up_c), (row, dn_c)):
+        signal(barrier, r, c)
+    pl.when(jnp.logical_not(at_last))(lambda: signal(barrier, row + 1, col))
 
     hops = doublings(n_row, n_col)
 
@@ -184,32 +219,26 @@
                 if k + 1 < len(hops):
                     call(k + 1)
 
-    sends = []
-
-    def remote(i, src, dst, to):
+    def remote(i, j, src, dst, to):
         return pltpu.make_async_remote_copy(
-            src_ref=src, dst_ref=dst, send_sem=h_send.at[i], recv_sem=h_recv.at[i],
+            src_ref=src, dst_ref=dst, send_sem=h_send.at[i], recv_sem=h_recv.at[j],
             device_id=to, device_id_type=MESH,
         )
 
-    def send(src, dst, to):
-        copy = remote(len(sends), src, dst, to)
-        copy.start()
-        sends.append(copy)
-        return copy
-
     def halo(piece, way):
-        if isinstance(piece, int) and piece == 0:
+        first, count = 0, 3
+        if isinstance(piece, int) and piece in (0, 3):
             rows = pl.ds(TILE, ny - 2 * TILE)
+            first, count = (1, 2) if piece else (0, 1)
+            piece = 0
         else:
             rows = pl.ds(pl.multiple_of((piece - 1) * (ny - TILE), TILE), TILE)
-        three = lambda at: pl.ds(at + 3 * way, 3)
+        planes = lambda at: pl.ds(at + 3 * way + first, count)
         to = lax.rem(row + 1 + way * (n_row - 2), n_row)
-        return remote(
-            2 + 2 * piece + way, yh.at[three(0), rows], q.at[three(nx), rows], (to, col)
-        )
+        return remote(0, piece, yh.at[planes(0), rows], q.at[planes(nx), rows], (to, col))
 
     with jax.named_scope("wz"):
+        alone = inner_twice(ny)
         fill_cyclic(wz_ref)
         sh[:, pl.ds(6, TILE - 6), :] = jnp.zeros((6, TILE - 6, nz), F32)
     def call_first():
@@ -219,73 +248,63 @@
     with jax.named_scope("barl"):
         pl.when(at_last)(call_first)
 
-    def prepare(way):
-        planes_of(way, lambda copy: copy.wait())
+    def prepare(way, flip):
+        landed(ext.at[pl.ds(0, len(needs[way]) - 1 + flip)], in_sem.at[1 + flip])
         made = (partials_low, partials_high)[way]
         planes = made(lambda i: ext[i], *((nx,) if way == 0 else ()))
         for i, plane in enumerate(planes):
             hs[3 * way + i] = plane
 
-    with jax.named_scope("hs0"):
-        for way in range(2):
-            pl.when(ways[0] == way)(lambda: prepare(way))
-        fetched[0].wait()
-    inside = 3 * (ny - 2 * TILE)
-    inner_rows = pl.ds(TILE, ny - 2 * TILE)
+    inside = ny - 2 * TILE
+    inner_rows = pl.ds(TILE, inside)
     outer_rows = (pl.ds(0, TILE), pl.ds(ny - TILE, TILE))
     plane_rows = lambda way: hs[pl.ds(3 * way, 3)].reshape(3 * ny, nz)
 
-    def lift_inner(way, data):
-        made = dot_pair(wx_ref[pl.ds(0, inside)], data)
-        yh[pl.ds(3 * way, 3), inner_rows, :] = made.reshape(3, ny - 2 * TILE, nz)
+    def lift_inner(way, data, first):
+        count = 3 - first
+        made = dot_pair(wx_ref[pl.ds(first * inside, count * inside)], data)
+        yh[pl.ds(3 * way + first, count), inner_rows, :] = made.reshape(count, inside, nz)
 
     def lift_outer(way, data):
-        made = dot_pair(wx_ref[pl.ds(inside, 6 * TILE)], data).reshape(3, 2 * TILE, nz)
+        made = dot_pair(wx_ref[pl.ds(3 * inside, 6 * TILE)], data).reshape(3, 2 * TILE, nz)
         for k, rows in enumerate(outer_rows):
             yh[pl.ds(3 * way, 3), rows, :] = made[:, k * TILE : (k + 1) * TILE, :]
 
+    with jax.named_scope("hs0"):
+        head_copy.wait()
     with jax.named_scope("lift0"):
-        lift_inner(ways[0], plane_rows(ways[0]))
+        yh[3 * ways[0], inner_rows, :] = dot_pair(alone, ext[head])
     with jax.named_scope("bar"):
         pl.when(at_first)(lambda: pl.semaphore_wait(barrier, 3))
         pl.when(jnp.logical_not(at_first | at_last))(lambda: pl.semaphore_wait(barrier, 4))
     halo(0, ways[0]).start()
+    with jax.named_scope("lift0b"):
+        for way in range(2):
+            pl.when(ways[0] == way)(lambda: prepare(way, 0))
+        fetched[0].wait()
+        lift_inner(ways[0], plane_rows(ways[0]), 1)
+    halo(3, ways[0]).start()
     with jax.named_scope("hs1"):
         for way in range(2):
-            pl.when(ways[1] == way)(lambda: prepare(way))
+            pl.when(ways[1] == way)(lambda: prepare(way, 1))
         for i in range(6):
             line = lambda j: hs[i, pl.ds(j, 1), :]
             for k, one in enumerate(partials_low(line, ny) + partials_high(line)):
                 sh[k, pl.ds(i, 1), :] = one
     lo, hi = pl.ds(0, 3), pl.ds(3, 3)
-    corner = [
-        send(sh.at[lo], ch.at[lo], (row, up_c)),
-        send(sh.at[hi], ch.at[hi], (row, dn_c)),
-    ]
-    inner, *outer = [[halo(piece, way) for way in range(2)] for piece in range(3)]
-    sends.extend(inner + outer[0] + outer[1])
+    for half_k, c in ((lo, up_c), (hi, dn_c)):
+        remote(1, 3, sh.at[half_k], ch.at[half_k], (row, c)).start()
     if hops:
         call(0)
-    loads = []
-    for i in range(3):
-        at = pl.ds(5 + i * ((nx - 11) // 3), (nx - 11) // 3)
-        if i == 2:
-            at = pl.ds(5 + 2 * ((nx - 11) // 3), nx - 11 - 2 * ((nx - 11) // 3))
-        loads.append(pltpu.make_async_copy(p_ref.at[at], ext.at[at], in_sem.at[10 + i]))
-    for i, plane in enumerate((3, nx - 5)):
-        at = pl.ds(plane, 1)
-        loads.append(pltpu.make_async_copy(p_ref.at[at], ext.at[at], in_sem.at[13 + i]))
-    for copy in loads:
-        copy.start()
-    for fetch in fetched[1:]:
-        fetch.start()
     with jax.named_scope("lift1"):
         lifted = dot2(plane_rows(ways[1]), wz_ref[...])
-        lift_inner(ways[1], lifted)
-    pl.when(jnp.logical_not(at_first))(lambda: halo(0, ways[1]).start())
-    with jax.named_scope("lift2"):
-        lift_outer(ways[1], lifted)
-        lift_outer(ways[0], dot2(plane_rows(ways[0]), wz_ref[...]))
+        lift_inner(ways[1], lifted, 0)
+
+    def second():
+        halo(0, ways[1]).start()
+        halo(3, ways[1]).start()
+
+    pl.when(jnp.logical_not(at_first))(second)
 
     far = lax.select(at_first, 1, lax.select(at_last, 0, odd_core))
     tail = (
@@ -293,7 +312,6 @@
         (1 + odd_core, odd_core * far + (1 - odd_core) * (1 - far)), (2, 1 - far),
     )
     groups = nx // grp
-    near = {}
 
     def z_group(g):
         at = pl.ds(g * grp, grp)
@@ -301,33 +319,32 @@
         got = dot2(wy_ref[...], v)
         q[at] = got[: grp * ny].reshape(grp, ny, nz)
         su[:, at, :] = got[grp * ny :].reshape(6, grp, nz)
-        near[g] = (
-            send(su.at[lo, at], u.at[lo, at], (row, up_c)),
-            send(su.at[hi, at], u.at[hi, at], (row, dn_c)),
-        )
+        for half_k, c in ((lo, up_c), (hi, dn_c)):
+            remote(2, 4 + g, su.at[half_k, at], u.at[half_k, at], (row, c)).start()
 
     with jax.named_scope("ld2"):
-        for copy in loads:
-            copy.wait()
+        landed(ext.at[pl.ds(0, nx - len(sum(needs, ())))], in_sem.at[3])
         for fetch in fetched[1:]:
             fetch.wait()
     order = (0, groups - 1, *range(1, groups - 1))
     with jax.named_scope("z"):
         for g in order[: groups // 2]:
             z_group(g)
+    with jax.named_scope("lift2"):
+        lift_outer(ways[1], lifted)
+        lift_outer(ways[0], dot2(plane_rows(ways[0]), wz_ref[...]))
     with jax.named_scope("last"):
 
         @pl.when(at_first)
         def _():
             pl.semaphore_wait(last_sem, 1)
-            halo(0, ways[1]).start()
+            second()
 
     relay(0)
     with jax.named_scope("z2"):
         z_group(order[groups // 2])
     with jax.named_scope("wait_corner"):
-        for copy in corner:
-            copy.wait_recv()
+        landed(ch, h_recv.at[3])
     with jax.named_scope("outer"):
         lifted = dot2(ch[...].reshape(6 * TILE, nz), wz_ref[...])
         more = dot_pair(wc_ref[...], lifted).reshape(6, 2 * TILE, nz)
@@ -413,13 +430,12 @@
         totals = x_stage(totals, False, 1, tiles - 1)
     relay(2)
     with jax.named_scope("wait_inner"):
-        for copy in inner:
-            copy.wait_recv()
+        landed(q.at[pl.ds(nx, 6), inner_rows], h_recv.at[0])
 
         def make_up(way):
             at = pl.ds(nx + 3 * way, 3)
-            raw = q[at, inner_rows, :].reshape(inside, nz)
-            q[at, inner_rows, :] = dot2(raw, wz_ref[...]).reshape(3, ny - 2 * TILE, nz)
+            raw = q[at, inner_rows, :].reshape(3 * inside, nz)
+            q[at, inner_rows, :] = dot2(raw, wz_ref[...]).reshape(3, inside, nz)
 
         pl.when(first_way(dn_r) == 0)(lambda: make_up(0))
         pl.when(first_way(up_r) == 1)(lambda: make_up(1))
@@ -427,8 +443,7 @@
         totals = x_stage(totals, True, 1, tiles - 1)
     for g in order:
         with jax.named_scope("wait_u"):
-            for copy in near[g]:
-                copy.wait_recv()
+            landed(u.at[:, pl.ds(g * grp, grp)], h_recv.at[4 + g])
         with jax.named_scope("u"):
             at = pl.ds(g * grp, grp)
             more = dot_pair(wu_ref[...], u[:, at, :].reshape(6 * grp, nz))
@@ -442,8 +457,7 @@
             totals = x_stage(totals, False, t, t + 1)
     for k, t in enumerate((0, tiles - 1)):
         with jax.named_scope("wait_outer"):
-            for copy in outer[k]:
-                copy.wait_recv()
+            landed(q.at[pl.ds(nx, 6), outer_rows[k]], h_recv.at[1 + k])
         with jax.named_scope("xouter"):
             totals = x_stage(totals, True, t, t + 1)
     with jax.named_scope("line"):
@@ -459,46 +473,38 @@
         part[...] = line
         slots[me] = line
 
-    def spread(r, c, t):
-        return pltpu.make_async_remote_copy(
-            src_ref=part, dst_ref=slots.at[me], send_sem=g_send.at[t],
-            recv_sem=g_recv.at[me], device_id=(r, c), device_id_type=MESH,
-        )
-
-    def gather(r, c, t):
-        return pltpu.make_async_remote_copy(
-            src_ref=part, dst_ref=slots.at[t], send_sem=g_send.at[t],
-            recv_sem=g_recv.at[t], device_id=(r, c), device_id_type=MESH,
-        )
+    def spread(r, c):
+        pltpu.make_async_remote_copy(
+            src_ref=part, dst_ref=slots.at[me], send_sem=g_sem.at[0],
+            recv_sem=g_sem.at[1], device_id=(r, c), device_id_type=MESH,
+        ).start()
 
     def peers(visit):
         if devices <= UNROLL:
             for j in (*range(1, n_row), 0):
                 for k in range(n_col):
                     if j or k:
-                        r, c = away_r(j), away_c(k)
-                        visit(r, c, r * n_col + c)
+                        visit(away_r(j), away_c(k))
             return
 
         @pl.loop(1, n_row)
         def _(j):
             @pl.loop(0, n_col)
             def _(k):
-                r, c = lax.rem(row + j, n_row), lax.rem(col + k, n_col)
-                visit(r, c, r * n_col + c)
+                visit(lax.rem(row + j, n_row), lax.rem(col + k, n_col))
 
         @pl.loop(1, n_col)
         def _(k):
-            c = lax.rem(col + k, n_col)
-            visit(row, c, row * n_col + c)
+            visit(row, lax.rem(col + k, n_col))
 
     with jax.named_scope("spread"):
-        peers(lambda r, c, t: spread(r, c, t).start())
+        peers(spread)
     with jax.named_scope("wsend"):
-        for copy in sends:
-            copy.wait_send()
+        for i, sent in enumerate((yh, sh, su)):
+            landed(sent, h_send.at[i])
     with jax.named_scope("gather"):
-        peers(lambda r, c, t: gather(r, c, t).wait())
+        for i in range(2):
+            landed(slots.at[pl.ds(0, devices - 1)], g_sem.at[i])
     mass_ref[...] = slots[...]
 
 
@@ -539,14 +545,15 @@
             planes.shape[1] * 2 * TILE, -1
         )
         core = np.r_[TILE : ny - TILE]
-        wx = np.concatenate([np.kron(np.eye(3), own[rows]) for rows in (core, rim)])
+        twice = lambda w: np.tile(w, 2)
+        wx = np.concatenate([twice(np.kron(np.eye(3), own[rows])) for rows in (core, rim)])
         wc, wu = spread(np.eye(TILE, 6)), spread(np.eye(grp))
-        twice = lambda w: np.tile(w, 2)
-        weights = [jnp.asarray(w, BF16) for w in (twice(wx), wy, twice(wc), twice(wu))]
+        wide = lambda w: np.pad(w, ((0, 0), (0, wy.shape[1] - w.shape[1])))
+        wall = np.concatenate([wy, wide(twice(wc)), wide(twice(wu))])
+        weights = [jnp.asarray(w, BF16) for w in (wx, wall)]
         vmem = pl.BlockSpec(memory_space=pltpu.VMEM)
         hbm = pl.BlockSpec(memory_space=pltpu.HBM)
         hops = len(doublings(n_row, n_col))
-        n_sends = 8 + 2 * (nx // grp)
         found = pl.pallas_call(
             functools.partial(kernel, n_row, n_col, grp),
             out_shape=(
@@ -570,12 +577,11 @@
                 pltpu.SMEM(group_map.shape, jnp.int32),
                 pltpu.VMEM((nz, nz), BF16),
                 *(pltpu.VMEM(w.shape, BF16) for w in weights),
-                pltpu.SemaphoreType.DMA((15,)),
+                pltpu.SemaphoreType.DMA((4,)),
                 pltpu.SemaphoreType.DMA((len(weights) + 2,)),
-                pltpu.SemaphoreType.DMA((n_sends,)),
-                pltpu.SemaphoreType.DMA((n_sends,)),
-                pltpu.SemaphoreType.DMA((devices,)),
-                pltpu.SemaphoreType.DMA((devices,)),
+                pltpu.SemaphoreType.DMA((3,)),
+                pltpu.SemaphoreType.DMA((4 + nx // grp,)),
+                pltpu.SemaphoreType.DMA((2,)),
                 pltpu.SemaphoreType.REGULAR((max(hops, 1),)),
                 pltpu.SemaphoreType.REGULAR,
             ],

time: 23.7 us -> 22.8 us (0.962)
  Pallas kernels: 22.9 us -> 22 us
    pallas_call x1, Pallas kernels: 21.5 us -> 20.6 us  [shards(): pl.pallas_call(functools.partial(kernel, n_row, n_col, grp), out_shape=(p...]
where the time goes in v4:
time: 22.8 us; the launch traced here: 22.6 us
  Pallas kernels  22 us (96%)
  between operations  0.64 us (3%)
    pallas_call x1, Pallas kernels, shards(): pl.pallas_call(functools.partial(kernel, n_row, n_col, grp), out_shape=(p...  20.6 us
    pallas_call x1, Pallas kernels, shards(): pl.pallas_call(deliver, out_shape=(pltpu.HBM((nx, ny, nz), F32), pltpu.HB...  1.35 us

profile of v4, /device:TPU:0, one launch (start us, length us, event | category | flops | bytes accessed | tf_op | source)
XLA Modules:
  0.0 22.6 jit_solution(13815610250528969058)
XLA Ops:
  0.6 20.6 %shard_map.68 = (f32[32,32,512]{2,1,0:T(8,128)S(1)}, f32[32,1,128]{2,1,0:T(1,128)S(1)}) custom-call(s32[1,1,2]{2,1,0:T(1,128)} %cut_hbm.1, s32[1,1,2]{2,1,0:T(1,128)} %map_hbm.1, f32[32,32,512]{2,1,0:T(8,128)} %p_ref.1, bf16[96,192]{1,0:T(8,128)(2,1)} %constant.4.clone.refs_0_, bf16[528,256]{1,0:T(8,128)(2,1)} %constant.5.clone.refs_1_), custom_call_target="tpu_custom_call" | custom-call | tf_op jit(solution)/shard_map/pallas_call | solution.py:557
  21.2 1.4 %shard_map.69 = (f32[32,32,512]{2,1,0:T(8,128)}, f32[4,16]{1,0:T(4,128)}) custom-call(f32[32,32,512]{2,1,0:T(8,128)S(1)} %get-tuple-element.6.c_ref, f32[32,1,128]{2,1,0:T(1,128)S(1)} %get-tuple-element.7.m_ref), custom_call_target="tpu_custom_call" | custom-call | tf_op jit(solution)/shard_map/pallas_call | solution.py:592

commit v5 on v4

--- a/solution.py
+++ b/solution.py
@@ -155,6 +155,10 @@
     def signal(sem, r, c):
         pl.semaphore_signal(sem, inc=1, device_id=(r, c), device_id_type=MESH)
 
+    for r, c in ((dn_r, col), (row, up_c), (row, dn_c)):
+        signal(barrier, r, c)
+    pl.when(jnp.logical_not(at_last))(lambda: signal(barrier, row + 1, col))
+
     fetched = [
         pltpu.make_async_copy(src, dst, w_sem.at[i])
         for i, (src, dst) in enumerate(
@@ -196,10 +200,6 @@
         copy.start()
     for fetch in fetched[1:]:
         fetch.start()
-
-    for r, c in ((dn_r, col), (row, up_c), (row, dn_c)):
-        signal(barrier, r, c)
-    pl.when(jnp.logical_not(at_last))(lambda: signal(barrier, row + 1, col))
 
     hops = doublings(n_row, n_col)
 
@@ -235,7 +235,8 @@
             rows = pl.ds(pl.multiple_of((piece - 1) * (ny - TILE), TILE), TILE)
         planes = lambda at: pl.ds(at + 3 * way + first, count)
         to = lax.rem(row + 1 + way * (n_row - 2), n_row)
-        return remote(0, piece, yh.at[planes(0), rows], q.at[planes(nx), rows], (to, col))
+        slot = piece if isinstance(piece, int) and piece == 0 else piece + way * (piece // 2)
+        return remote(0, slot, yh.at[planes(0), rows], q.at[planes(nx), rows], (to, col))
 
     with jax.named_scope("wz"):
         alone = inner_twice(ny)
@@ -293,7 +294,7 @@
                 sh[k, pl.ds(i, 1), :] = one
     lo, hi = pl.ds(0, 3), pl.ds(3, 3)
     for half_k, c in ((lo, up_c), (hi, dn_c)):
-        remote(1, 3, sh.at[half_k], ch.at[half_k], (row, c)).start()
+        remote(1, 4, sh.at[half_k], ch.at[half_k], (row, c)).start()
     if hops:
         call(0)
     with jax.named_scope("lift1"):
@@ -320,7 +321,7 @@
         q[at] = got[: grp * ny].reshape(grp, ny, nz)
         su[:, at, :] = got[grp * ny :].reshape(6, grp, nz)
         for half_k, c in ((lo, up_c), (hi, dn_c)):
-            remote(2, 4 + g, su.at[half_k, at], u.at[half_k, at], (row, c)).start()
+            remote(2, 5 + g, su.at[half_k, at], u.at[half_k, at], (row, c)).start()
 
     with jax.named_scope("ld2"):
         landed(ext.at[pl.ds(0, nx - len(sum(needs, ())))], in_sem.at[3])
@@ -344,7 +345,7 @@
     with jax.named_scope("z2"):
         z_group(order[groups // 2])
     with jax.named_scope("wait_corner"):
-        landed(ch, h_recv.at[3])
+        landed(ch, h_recv.at[4])
     with jax.named_scope("outer"):
         lifted = dot2(ch[...].reshape(6 * TILE, nz), wz_ref[...])
         more = dot_pair(wc_ref[...], lifted).reshape(6, 2 * TILE, nz)
@@ -363,7 +364,7 @@
     odd = lambda axis: lax.broadcasted_iota(jnp.int32, (TILE, LANES), axis) % 2
     mixed = (odd(0) + odd(1)) > 0
 
-    def x_stage(totals, edges, first, last):
+    def x_stage(totals, edges, first, last, sides=(1, 0)):
         totals = list(totals)
         for z in range(zb):
             cuts = jnp.full((TILE, LANES), -cut_ref[0, 0, z], jnp.int32)
@@ -406,12 +407,13 @@
                             put(2 * j + 1, d[j])
                             if j >= 4:
                                 smooth(d, j - 1)
-                    else:
+                    if edges and 0 in sides:
                         d = {j: out_ref[2 * j + 1, rows, lanes] for j in (1, 2, 3)}
                         d |= {j: detail(j) for j in (-2, -1, 0)}
                         put(1, d[0])
                         for j in (0, 1, 2):
                             smooth(d, j)
+                    if edges and 1 in sides:
                         d = {j: out_ref[2 * j + 1, rows, lanes] for j in range(half - 5, half - 2)}
                         d |= {j: detail(j) for j in range(half - 2, half + 1)}
                         for j in (half - 2, half - 1):
@@ -443,7 +445,7 @@
         totals = x_stage(totals, True, 1, tiles - 1)
     for g in order:
         with jax.named_scope("wait_u"):
-            landed(u.at[:, pl.ds(g * grp, grp)], h_recv.at[4 + g])
+            landed(u.at[:, pl.ds(g * grp, grp)], h_recv.at[5 + g])
         with jax.named_scope("u"):
             at = pl.ds(g * grp, grp)
             more = dot_pair(wu_ref[...], u[:, at, :].reshape(6 * grp, nz))
@@ -455,11 +457,15 @@
     with jax.named_scope("xin2"):
         for t in (0, tiles - 1):
             totals = x_stage(totals, False, t, t + 1)
-    for k, t in enumerate((0, tiles - 1)):
+    with jax.named_scope("wait_outer"):
+        landed(q.at[pl.ds(nx, 6), outer_rows[0]], h_recv.at[1])
+    with jax.named_scope("xouter"):
+        totals = x_stage(totals, True, 0, 1)
+    for way in (1, 0):
         with jax.named_scope("wait_outer"):
-            landed(q.at[pl.ds(nx, 6), outer_rows[k]], h_recv.at[1 + k])
+            landed(q.at[pl.ds(nx + 3 * way, 3), outer_rows[1]], h_recv.at[2 + way])
         with jax.named_scope("xouter"):
-            totals = x_stage(totals, True, t, t + 1)
+            totals = x_stage(totals, True, tiles - 1, tiles, (way,))
     with jax.named_scope("line"):
         rows = zb * n_lev
         lane, at = (lax.broadcasted_iota(jnp.int32, (rows, LANES), axis) for axis in (1, 0))
@@ -580,7 +586,7 @@
                 pltpu.SemaphoreType.DMA((4,)),
                 pltpu.SemaphoreType.DMA((len(weights) + 2,)),
                 pltpu.SemaphoreType.DMA((3,)),
-                pltpu.SemaphoreType.DMA((4 + nx // grp,)),
+                pltpu.SemaphoreType.DMA((5 + nx // grp,)),
                 pltpu.SemaphoreType.DMA((2,)),
                 pltpu.SemaphoreType.REGULAR((max(hops, 1),)),
                 pltpu.SemaphoreType.REGULAR,
@@ -598,7 +604,7 @@
             out_specs=(hbm, hbm),
             scratch_shapes=[
                 pltpu.VMEM((len(LEVELS), GROUPS), F32),
-                pltpu.SemaphoreType.DMA((2,)),
+                pltpu.SemaphoreType.DMA((1,)),
                 pltpu.SemaphoreType.DMA,
             ],
             compiler_params=pltpu.CompilerParams(vmem_limit_bytes=2**20),

time: 22.8 us -> 22.7 us (level)
  no operation moved by 1% of the time
where the time goes in v5:
time: 22.7 us; the launch traced here: 22.5 us
  Pallas kernels  21.9 us (96%)
  between operations  0.64 us (3%)
    pallas_call x1, Pallas kernels, shards(): pl.pallas_call(functools.partial(kernel, n_row, n_col, grp), out_shape=(p...  20.5 us
    pallas_call x1, Pallas kernels, shards(): pl.pallas_call(deliver, out_shape=(pltpu.HBM((nx, ny, nz), F32), pltpu.HB...  1.35 us

profile of v5, /device:TPU:0, one launch (start us, length us, event | category | flops | bytes accessed | tf_op | source)
XLA Modules:
  0.0 22.5 jit_solution(14442750179537810713)
XLA Ops:
  0.6 20.5 %shard_map.68 = (f32[32,32,512]{2,1,0:T(8,128)S(1)}, f32[32,1,128]{2,1,0:T(1,128)S(1)}) custom-call(s32[1,1,2]{2,1,0:T(1,128)} %cut_hbm.1, s32[1,1,2]{2,1,0:T(1,128)} %map_hbm.1, f32[32,32,512]{2,1,0:T(8,128)} %p_ref.1, bf16[96,192]{1,0:T(8,128)(2,1)} %constant.4.clone.refs_0_, bf16[528,256]{1,0:T(8,128)(2,1)} %constant.5.clone.refs_1_), custom_call_target="tpu_custom_call" | custom-call | tf_op jit(solution)/shard_map/pallas_call | solution.py:563
  21.2 1.3 %shard_map.69 = (f32[32,32,512]{2,1,0:T(8,128)}, f32[4,16]{1,0:T(4,128)}) custom-call(f32[32,32,512]{2,1,0:T(8,128)S(1)} %get-tuple-element.6.c_ref, f32[32,1,128]{2,1,0:T(1,128)S(1)} %get-tuple-element.7.m_ref), custom_call_target="tpu_custom_call" | custom-call | tf_op jit(solution)/shard_map/pallas_call | solution.py:598

commit v6 on v5

--- a/solution.py
+++ b/solution.py
@@ -131,10 +131,10 @@
 def kernel(n_row, n_col, grp, cut_hbm, map_hbm, p_ref, *refs):
     weights, refs = refs[:2], refs[2:]
     out_ref, mass_ref = refs[:2]
-    ext, q, hs, yh, sh, ch, su, u, part, slots, cut_ref, map_ref, wz_ref = refs[2:15]
-    held = refs[15:17]
+    ext, q, hs, yh, ch, su, u, part, slots, block_ref, wz_ref = refs[2:13]
+    held = refs[13:15]
     wx_ref, wall_ref = held
-    in_sem, w_sem, h_send, h_recv, g_sem, hop_sem, last_sem = refs[17:]
+    in_sem, w_sem, h_send, h_recv, g_sem, hop_sem, last_sem = refs[15:]
     nx, ny, nz = p_ref.shape
     half = nx // 2
     tall = grp * ny + 6 * grp
@@ -161,14 +161,12 @@
 
     fetched = [
         pltpu.make_async_copy(src, dst, w_sem.at[i])
-        for i, (src, dst) in enumerate(
-            zip((*weights, cut_hbm, map_hbm), (*held, cut_ref, map_ref), strict=True)
-        )
+        for i, (src, dst) in enumerate(zip(weights, held, strict=True))
     ]
     odd_core = lax.rem(col, 2)
 
     def first_way(r):
-        return lax.select(r == 0, 0, lax.select(r == top, odd_core, 1 - odd_core))
+        return lax.select(r == 0, 0, odd_core)
 
     ways = (first_way(row), 1 - first_way(row))
     needs = ((nx - 2, nx - 1, nx - 4, nx - 3, nx - 6), (0, 2, 1, 4))
@@ -200,6 +198,8 @@
         copy.start()
     for fetch in fetched[1:]:
         fetch.start()
+    for src, i in ((cut_hbm, 0), (map_hbm, 1)):
+        pltpu.make_async_copy(src, block_ref.at[pl.ds(i, 1)], w_sem.at[2]).start()
 
     hops = doublings(n_row, n_col)
 
@@ -241,7 +241,7 @@
     with jax.named_scope("wz"):
         alone = inner_twice(ny)
         fill_cyclic(wz_ref)
-        sh[:, pl.ds(6, TILE - 6), :] = jnp.zeros((6, TILE - 6, nz), F32)
+        su[:, pl.ds(nx + 6, TILE - 6), :] = jnp.zeros((6, TILE - 6, nz), F32)
     def call_first():
         pl.semaphore_wait(barrier, 4)
         signal(last_sem, 0, col)
@@ -291,10 +291,10 @@
         for i in range(6):
             line = lambda j: hs[i, pl.ds(j, 1), :]
             for k, one in enumerate(partials_low(line, ny) + partials_high(line)):
-                sh[k, pl.ds(i, 1), :] = one
+                su[k, pl.ds(nx + i, 1), :] = one
     lo, hi = pl.ds(0, 3), pl.ds(3, 3)
     for half_k, c in ((lo, up_c), (hi, dn_c)):
-        remote(1, 4, sh.at[half_k], ch.at[half_k], (row, c)).start()
+        remote(1, 4, su.at[half_k, pl.ds(nx, TILE)], ch.at[half_k], (row, c)).start()
     if hops:
         call(0)
     with jax.named_scope("lift1"):
@@ -313,6 +313,7 @@
         (1 + odd_core, odd_core * far + (1 - odd_core) * (1 - far)), (2, 1 - far),
     )
     groups = nx // grp
+    order = (0, groups - 1, *range(1, groups - 1))
 
     def z_group(g):
         at = pl.ds(g * grp, grp)
@@ -321,19 +322,16 @@
         q[at] = got[: grp * ny].reshape(grp, ny, nz)
         su[:, at, :] = got[grp * ny :].reshape(6, grp, nz)
         for half_k, c in ((lo, up_c), (hi, dn_c)):
-            remote(2, 5 + g, su.at[half_k, at], u.at[half_k, at], (row, c)).start()
+            remote(1, 5 + (g == order[-1]), su.at[half_k, at], u.at[half_k, at], (row, c)).start()
 
     with jax.named_scope("ld2"):
         landed(ext.at[pl.ds(0, nx - len(sum(needs, ())))], in_sem.at[3])
         for fetch in fetched[1:]:
             fetch.wait()
-    order = (0, groups - 1, *range(1, groups - 1))
+        landed(block_ref, w_sem.at[2])
     with jax.named_scope("z"):
         for g in order[: groups // 2]:
             z_group(g)
-    with jax.named_scope("lift2"):
-        lift_outer(ways[1], lifted)
-        lift_outer(ways[0], dot2(plane_rows(ways[0]), wz_ref[...]))
     with jax.named_scope("last"):
 
         @pl.when(at_first)
@@ -341,6 +339,9 @@
             pl.semaphore_wait(last_sem, 1)
             second()
 
+    with jax.named_scope("lift2"):
+        lift_outer(ways[1], lifted)
+        lift_outer(ways[0], dot2(plane_rows(ways[0]), wz_ref[...]))
     relay(0)
     with jax.named_scope("z2"):
         z_group(order[groups // 2])
@@ -358,7 +359,7 @@
             z_group(g)
     relay(1)
 
-    zb = cut_ref.shape[2]
+    zb = block_ref.shape[2]
     width = nz // zb
     n_lev = len(LEVELS)
     odd = lambda axis: lax.broadcasted_iota(jnp.int32, (TILE, LANES), axis) % 2
@@ -367,7 +368,7 @@
     def x_stage(totals, edges, first, last, sides=(1, 0)):
         totals = list(totals)
         for z in range(zb):
-            cuts = jnp.full((TILE, LANES), -cut_ref[0, 0, z], jnp.int32)
+            cuts = jnp.full((TILE, LANES), -block_ref[0, 0, z], jnp.int32)
             scale = jnp.exp2(cuts.astype(F32))
             limits = [level * scale for level in LEVELS]
 
@@ -445,7 +446,9 @@
         totals = x_stage(totals, True, 1, tiles - 1)
     for g in order:
         with jax.named_scope("wait_u"):
-            landed(u.at[:, pl.ds(g * grp, grp)], h_recv.at[5 + g])
+            if g in (order[0], order[-1]):
+                count = 1 if g == order[-1] else groups - 1
+                landed(u.at[:, pl.ds(0, count * grp)], h_recv.at[6 - (count > 1)])
         with jax.named_scope("u"):
             at = pl.ds(g * grp, grp)
             more = dot_pair(wu_ref[...], u[:, at, :].reshape(6 * grp, nz))
@@ -469,9 +472,9 @@
     with jax.named_scope("line"):
         rows = zb * n_lev
         lane, at = (lax.broadcasted_iota(jnp.int32, (rows, LANES), axis) for axis in (1, 0))
-        group = jnp.full((rows, LANES), map_ref[0, 0, 0], jnp.int32)
+        group = jnp.full((rows, LANES), block_ref[1, 0, 0], jnp.int32)
         for z in range(1, zb):
-            group = jnp.where(at >= z * n_lev, map_ref[0, 0, z], group)
+            group = jnp.where(at >= z * n_lev, block_ref[1, 0, z], group)
         sums = jnp.concatenate([jnp.sum(total, axis=0, keepdims=True) for total in totals], 0)
         mass = jnp.sum(sums, axis=1, keepdims=True) / (nx * ny * width)
         line = jnp.where(lane == at % n_lev * GROUPS + group, mass, 0.0)
@@ -506,7 +509,7 @@
     with jax.named_scope("spread"):
         peers(spread)
     with jax.named_scope("wsend"):
-        for i, sent in enumerate((yh, sh, su)):
+        for i, sent in enumerate((yh, su)):
             landed(sent, h_send.at[i])
     with jax.named_scope("gather"):
         for i in range(2):
@@ -574,19 +577,17 @@
                 pltpu.VMEM((6, ny, nz), F32),
                 pltpu.VMEM((6, ny, nz), F32),
                 pltpu.VMEM((6, TILE, nz), F32),
-                pltpu.VMEM((6, TILE, nz), F32),
-                pltpu.VMEM((6, nx, nz), F32),
+                pltpu.VMEM((6, nx + TILE, nz), F32),
                 pltpu.VMEM((6, nx, nz), F32),
                 pltpu.VMEM((1, LANES), F32),
                 pltpu.VMEM((devices, 1, LANES), F32),
-                pltpu.SMEM(cut_exponent.shape, jnp.int32),
-                pltpu.SMEM(group_map.shape, jnp.int32),
+                pltpu.SMEM((2, *cut_exponent.shape[1:]), jnp.int32),
                 pltpu.VMEM((nz, nz), BF16),
                 *(pltpu.VMEM(w.shape, BF16) for w in weights),
                 pltpu.SemaphoreType.DMA((4,)),
-                pltpu.SemaphoreType.DMA((len(weights) + 2,)),
-                pltpu.SemaphoreType.DMA((3,)),
-                pltpu.SemaphoreType.DMA((5 + nx // grp,)),
+                pltpu.SemaphoreType.DMA((len(weights) + 1,)),
+                pltpu.SemaphoreType.DMA((2,)),
+                pltpu.SemaphoreType.DMA((7,)),
                 pltpu.SemaphoreType.DMA((2,)),
                 pltpu.SemaphoreType.REGULAR((max(hops, 1),)),
                 pltpu.SemaphoreType.REGULAR,

time: 22.7 us -> 22.6 us (level)
  no operation moved by 1% of the time
where the time goes in v6:
time: 22.6 us; the launch traced here: 22.4 us
  Pallas kernels  21.8 us (96%)
  between operations  0.64 us (3%)
    pallas_call x1, Pallas kernels, shards(): pl.pallas_call(functools.partial(kernel, n_row, n_col, grp), out_shape=(p...  20.4 us
    pallas_call x1, Pallas kernels, shards(): pl.pallas_call(deliver, out_shape=(pltpu.HBM((nx, ny, nz), F32), pltpu.HB...  1.35 us

profile of v6, /device:TPU:0, one launch (start us, length us, event | category | flops | bytes accessed | tf_op | source)
XLA Modules:
  0.0 22.4 jit_solution(1847514513780692586)
XLA Ops:
  0.6 20.4 %shard_map.68 = (f32[32,32,512]{2,1,0:T(8,128)S(1)}, f32[32,1,128]{2,1,0:T(1,128)S(1)}) custom-call(s32[1,1,2]{2,1,0:T(1,128)} %cut_hbm.1, s32[1,1,2]{2,1,0:T(1,128)} %map_hbm.1, f32[32,32,512]{2,1,0:T(8,128)} %p_ref.1, bf16[96,192]{1,0:T(8,128)(2,1)} %constant.4.clone.refs_0_, bf16[528,256]{1,0:T(8,128)(2,1)} %constant.5.clone.refs_1_), custom_call_target="tpu_custom_call" | custom-call | tf_op jit(solution)/shard_map/pallas_call | solution.py:566
  21.1 1.3 %shard_map.69 = (f32[32,32,512]{2,1,0:T(8,128)}, f32[4,16]{1,0:T(4,128)}) custom-call(f32[32,32,512]{2,1,0:T(8,128)S(1)} %get-tuple-element.6.c_ref, f32[32,1,128]{2,1,0:T(1,128)S(1)} %get-tuple-element.7.m_ref), custom_call_target="tpu_custom_call" | custom-call | tf_op jit(solution)/shard_map/pallas_call | solution.py:599

commit v7 on v6

--- a/solution.py
+++ b/solution.py
@@ -352,8 +352,10 @@
         more = dot_pair(wc_ref[...], lifted).reshape(6, 2 * TILE, nz)
         for k, rows in enumerate(outer_rows):
             yh[:, rows, :] += more[:, k * TILE : (k + 1) * TILE, :]
-        for piece, way in tail:
+        for piece, way in tail[:3]:
             halo(piece, way).start()
+        last_piece = halo(*tail[3])
+        pl.when(odd_core == 0)(last_piece.start)
     with jax.named_scope("z3"):
         for g in order[groups // 2 + 1 :]:
             z_group(g)
@@ -455,6 +457,7 @@
             more = more.reshape(grp, 2 * TILE, nz)
             for k, rows in enumerate(outer_rows):
                 q[at, rows, :] += more[:, k * TILE : (k + 1) * TILE, :]
+    pl.when(odd_core == 1)(lambda: halo(*tail[3]).start())
     for k in range(3, len(hops)):
         relay(k)
     with jax.named_scope("xin2"):

time: 22.6 us -> 22.6 us (level)
  no operation moved by 1% of the time
where the time goes in v7:
time: 22.6 us; the launch traced here: 22.4 us
  Pallas kernels  21.8 us (96%)
  between operations  0.64 us (3%)
    pallas_call x1, Pallas kernels, shards(): pl.pallas_call(functools.partial(kernel, n_row, n_col, grp), out_shape=(p...  20.4 us
    pallas_call x1, Pallas kernels, shards(): pl.pallas_call(deliver, out_shape=(pltpu.HBM((nx, ny, nz), F32), pltpu.HB...  1.35 us

profile of v7, /device:TPU:0, one launch (start us, length us, event | category | flops | bytes accessed | tf_op | source)
XLA Modules:
  0.0 22.4 jit_solution(9606604966362379447)
XLA Ops:
  0.6 20.4 %shard_map.68 = (f32[32,32,512]{2,1,0:T(8,128)S(1)}, f32[32,1,128]{2,1,0:T(1,128)S(1)}) custom-call(s32[1,1,2]{2,1,0:T(1,128)} %cut_hbm.1, s32[1,1,2]{2,1,0:T(1,128)} %map_hbm.1, f32[32,32,512]{2,1,0:T(8,128)} %p_ref.1, bf16[96,192]{1,0:T(8,128)(2,1)} %constant.4.clone.refs_0_, bf16[528,256]{1,0:T(8,128)(2,1)} %constant.5.clone.refs_1_), custom_call_target="tpu_custom_call" | custom-call | tf_op jit(solution)/shard_map/pallas_call | solution.py:569
  21.1 1.3 %shard_map.69 = (f32[32,32,512]{2,1,0:T(8,128)}, f32[4,16]{1,0:T(4,128)}) custom-call(f32[32,32,512]{2,1,0:T(8,128)S(1)} %get-tuple-element.6.c_ref, f32[32,1,128]{2,1,0:T(1,128)S(1)} %get-tuple-element.7.m_ref), custom_call_target="tpu_custom_call" | custom-call | tf_op jit(solution)/shard_map/pallas_call | solution.py:602
